TPU v7x, 32 devices: a whole 2x2x4 slice. The times are simulated.
32 devices in a mesh: gz: 8 (over z, y), gy: 4 (over x, core).
Axes of the slice: x: 2, y: 2, z: 4, core: 2. Of those that a mesh axis runs over, the one named last changes fastest.
Arguments:
- right_side: float32 [8, 16, 256, 512], P(None, 'gz', 'gy'), may hold values from -8 to 8
- diagonal: float32 [16, 256, 512], P('gz', 'gy'), may hold values from 0.1 to 4
Outputs:
- solution: float32 [8, 16, 256, 512], P(None, 'gz', 'gy')
- hessenberg: float32 [24, 32], replicated
All inputs are finite; a program needn't handle non-finite values.
Results may differ from a plain program's by a relative error of at most 0.0003.
Values sent between devices are 32-bit elements; how exact they have to be, the bound alone decides.
A program may use at most 64 MiB of HBM per device.

v0:
```python
import functools

import jax
import jax.numpy as jnp
from jax import lax
from jax.experimental import pallas as pl
from jax.experimental.pallas import tpu as pltpu
from jax.sharding import PartitionSpec as P

ITERS = 3
CENTRE = 7.5
SCALE = 0.25
CHUNKS = 4
EARLY = 3
MESH = pl.DeviceIdType.MESH
HIGH = lax.Precision.HIGHEST


def nt_dot(left, right):
    return lax.dot_general(
        left, right, (((1,), (1,)), ((), ())), precision=HIGH, preferred_element_type=jnp.float32
    )


def dot(left, right):
    return jnp.dot(left, right, precision=HIGH, preferred_element_type=jnp.float32)


def kernel(
    r_ref, d_ref, out_ref, hess_ref,
    k0, k1, k2, k3, diag, ret1, ret2, held, ys, yh, acc, mine, slots1, part, slots2, splat,
    x_s, x_r, d_s, d_r, z_s, z_r, y_s, y_r, b_s, b_r, l_s, l_r, g1_s, g1_r, g2_s, g2_r,
):
    blk, lay, rows, nx = r_ref.shape
    half, group_lay = rows // 2, 2 * lay
    vc = blk // CHUNKS
    n_z, n_y = lax.axis_size("gz"), lax.axis_size("gy")
    gz, gy = lax.axis_index("gz"), lax.axis_index("gy")
    p, group = gz % 2, gz // 2
    h = (p + gy) % 2
    partner = gz + 1 - 2 * p
    hs = pl.multiple_of(h * half, half)
    os = pl.multiple_of((1 - h) * half, half)
    mine_at = p * lay
    theirs_at = (1 - p) * lay
    below, above = group > 0, group < n_z // 2 - 1
    place = 2 * gy + h
    before, after = place > 0, place < 2 * n_y - 1
    prev_dev = (gz + h * (partner - gz), gy - (1 - h))
    next_dev = (gz + (1 - h) * (partner - gz), gy + h)
    basis = (k0, k1, k2, k3)
    edge = (lay - 1) * p

    def remote(src, dst, send, recv, dev):
        return pltpu.make_async_remote_copy(
            src_ref=src, dst_ref=dst, send_sem=send, recv_sem=recv, device_id=dev,
            device_id_type=MESH,
        )

    @pl.when(jnp.logical_not(below))
    def _():
        for k in (k0, k1, k2):
            k[:, 0] = jnp.zeros((blk, half, nx), jnp.float32)

    @pl.when(jnp.logical_not(above))
    def _():
        for k in (k0, k1, k2):
            k[:, group_lay + 1] = jnp.zeros((blk, half, nx), jnp.float32)

    @pl.when(jnp.logical_not(before))
    def _():
        yh[:, 0] = jnp.zeros((ITERS,) + yh.shape[2:], jnp.float32)

    @pl.when(jnp.logical_not(after))
    def _():
        yh[:, 1] = jnp.zeros((ITERS,) + yh.shape[2:], jnp.float32)

    barrier = pltpu.get_barrier_semaphore()
    for step in range(1, n_z):
        pl.semaphore_signal(
            barrier, inc=1, device_id=((gz + step) % n_z, gy), device_id_type=MESH
        )
    for step in range(1, n_y):
        pl.semaphore_signal(
            barrier, inc=1, device_id=(gz, (gy + step) % n_y), device_id_type=MESH
        )
    pl.semaphore_wait(barrier, n_z + n_y - 2)

    def exchange(which, ch):
        layer = edge + which * (1 - 2 * p)
        vs = pl.ds(ch * vc, vc)
        return remote(
            r_ref.at[vs, pl.ds(layer, 1), pl.ds(os, half)],
            k0.at[vs, pl.ds(1 + mine_at + layer, 1)],
            x_s.at[which, ch], x_r.at[which, ch], (partner, gy),
        )

    def z_from_rhs(ch, direction):
        vs = pl.ds(ch * vc, vc)
        if direction == 0:
            dst, dev = k0.at[vs, pl.ds(group_lay + 1, 1)], (gz - 2, gy)
        else:
            dst, dev = k0.at[vs, pl.ds(0, 1)], (gz + 2, gy)
        return remote(
            r_ref.at[vs, pl.ds(edge, 1), pl.ds(hs, half)], dst,
            z_s.at[0, direction, ch], z_r.at[0, direction, ch], dev,
        )

    def z_copy(j, ch, direction):
        vs = pl.ds(ch * vc, vc)
        k = basis[j]
        if direction == 0:
            src, dst, dev = k.at[vs, pl.ds(1, 1)], k.at[vs, pl.ds(group_lay + 1, 1)], (gz - 2, gy)
        else:
            src, dst, dev = k.at[vs, pl.ds(group_lay, 1)], k.at[vs, pl.ds(0, 1)], (gz + 2, gy)
        return remote(src, dst, z_s.at[j, direction, ch], z_r.at[j, direction, ch], dev)

    def y_copy(j, ch, side):
        vs = pl.ds(ch * vc, vc)
        dev = prev_dev if side == 0 else next_dev
        return remote(
            ys.at[j, side, vs], yh.at[j, 1 - side, vs],
            y_s.at[j, side, ch], y_r.at[j, 1 - side, ch], dev,
        )

    def y_wait_recv(j, ch, side):
        vs = pl.ds(ch * vc, vc)
        remote(
            ys.at[j, side, vs], yh.at[j, side, vs], y_s.at[j, side, ch], y_r.at[j, side, ch],
            (partner, gy),
        ).wait_recv()

    early = ret1.shape[2]
    late = half - early

    def back_copy(j, ch, layer):
        vs = pl.ds(ch * vc, vc)
        dst = (ret1, ret2)[j - 1]
        return remote(
            basis[j].at[vs, pl.ds(1 + theirs_at + layer, 1), pl.ds(0, early)],
            dst.at[vs, pl.ds(layer, 1)],
            b_s.at[j - 1, layer, ch], b_r.at[j - 1, layer, ch], (partner, gy),
        )

    def late_copy(layer):
        return remote(
            held.at[:, pl.ds(layer, 1)],
            out_ref.at[:, pl.ds(layer, 1), pl.ds(pl.multiple_of(hs + early, 8), late)],
            l_s.at[layer], l_r.at[layer], (partner, gy),
        )

    diag_copy = remote(
        d_ref.at[:, pl.ds(os, half)], diag.at[pl.ds(mine_at, lay)], d_s, d_r, (partner, gy)
    )

    def chunks(body):
        def run(ch, carry):
            body(ch)
            return carry

        lax.fori_loop(0, CHUNKS, run, 0)

    def first(ch):
        exchange(0, ch).start()

        @pl.when((p == 0) & below)
        def _():
            z_from_rhs(ch, 0).start()

        @pl.when((p == 1) & above)
        def _():
            z_from_rhs(ch, 1).start()

    chunks(first)
    chunks(lambda ch: exchange(1, ch).start())
    diag_copy.start()

    def own(v, carry):
        k0[v, pl.ds(1 + mine_at, lay)] = r_ref[v, :, pl.ds(hs, half)]
        return carry

    lax.fori_loop(0, blk, own, 0)
    diag[pl.ds(mine_at, lay)] = d_ref[:, pl.ds(hs, half)]

    lanes = nx // 128

    def gram(moment, left, right, l_at, r_at, layers, height):
        tiles = height // 8
        pairs = [(a, b) for a in range(blk) for b in range(a, blk)]

        def run(i, sums):
            layer, at = i // tiles, pl.multiple_of((i % tiles) * 8, 8)
            for lane in range(lanes):
                cols = pl.ds(lane * 128, 128)
                x = [left[v, l_at + layer, pl.ds(at, 8), cols] for v in range(blk)]
                y = x if left is right else [
                    right[v, r_at + layer, pl.ds(at, 8), cols] for v in range(blk)
                ]
                sums = tuple(s + x[a] * y[b] for s, (a, b) in zip(sums, pairs))
            return sums

        zero = jnp.zeros((8, 128), jnp.float32)
        sums = lax.fori_loop(0, layers * tiles, run, (zero,) * len(pairs))
        for s, (a, b) in zip(sums, pairs):
            line = jnp.sum(s, axis=0, keepdims=True)
            at = (moment * blk + a) * blk + b
            acc[at:at + 1] = line
            if a != b:
                at = (moment * blk + b) * blk + a
                acc[at:at + 1] = line

    acc[7 * blk * blk:] = jnp.zeros((acc.shape[0] - 7 * blk * blk, 128), jnp.float32)
    gram(0, r_ref, r_ref, 0, 0, lay, rows)

    def relay(ch):
        exchange_in = remote(
            r_ref.at[pl.ds(0, vc), pl.ds(0, 1), pl.ds(os, half)],
            k0.at[pl.ds(ch * vc, vc), pl.ds(1 + (group_lay - 1) * (1 - p), 1)],
            x_s.at[0, ch], x_r.at[0, ch], (partner, gy),
        )
        exchange_in.wait_recv()

        @pl.when((p == 0) & above)
        def _():
            z_copy(0, ch, 1).start()

        @pl.when((p == 1) & below)
        def _():
            z_copy(0, ch, 0).start()

    chunks(relay)

    def stage_rows(j, v, layer, value):
        ys[j, 0, v, layer:layer + 1] = value[:1]
        ys[j, 1, v, layer:layer + 1] = value[half - 1:]

    def start_rows(j, ch):
        @pl.when(before)
        def _():
            y_copy(j, ch, 0).start()

        @pl.when(after)
        def _():
            y_copy(j, ch, 1).start()

    def arrived(ch):
        remote(
            r_ref.at[pl.ds(0, vc), pl.ds(0, 1), pl.ds(os, half)],
            k0.at[pl.ds(ch * vc, vc), pl.ds(1 + lay - p, 1)],
            x_s.at[1, ch], x_r.at[1, ch], (partner, gy),
        ).wait_recv()

        def run(v, carry):
            for layer in range(group_lay):
                stage_rows(0, v, layer, k0[v, 1 + layer])
            return carry

        lax.fori_loop(ch * vc, (ch + 1) * vc, run, 0)
        start_rows(0, ch)

    chunks(arrived)
    remote(
        d_ref.at[:, pl.ds(os, half)], diag.at[pl.ds(theirs_at, lay)], d_s, d_r, (partner, gy)
    ).wait_recv()

    row_at = lax.broadcasted_iota(jnp.int32, (half, nx), 0)
    col_at = lax.broadcasted_iota(jnp.int32, (half, nx), 1)

    def step(j):
        src, dst = basis[j], basis[j + 1]
        shift = 0 if j == 2 else 1

        def apply(ch):
            @pl.when(below)
            def _():
                vs = pl.ds(ch * vc, vc)
                remote(
                    src.at[vs, pl.ds(1, 1)], src.at[vs, pl.ds(0, 1)],
                    z_s.at[j, 1, ch], z_r.at[j, 1, ch], (partner, gy),
                ).wait_recv()

            @pl.when(above)
            def _():
                vs = pl.ds(ch * vc, vc)
                remote(
                    src.at[vs, pl.ds(1, 1)], src.at[vs, pl.ds(group_lay + 1, 1)],
                    z_s.at[j, 0, ch], z_r.at[j, 0, ch], (partner, gy),
                ).wait_recv()

            @pl.when(before)
            def _():
                y_wait_recv(j, ch, 0)

            @pl.when(after)
            def _():
                y_wait_recv(j, ch, 1)

            def run(v, carry):
                for layer in range(group_lay):
                    here = src[v, 1 + layer]
                    near = src[v, layer] + src[v, 2 + layer]
                    up = jnp.where(
                        row_at == 0, yh[j, 0, v, layer:layer + 1], pltpu.roll(here, 1, 0)
                    )
                    down = jnp.where(
                        row_at == half - 1, yh[j, 1, v, layer:layer + 1],
                        pltpu.roll(here, half - 1, 0),
                    )
                    left = jnp.where(col_at == 0, 0.0, pltpu.roll(here, 1, 1))
                    right = jnp.where(col_at == nx - 1, 0.0, pltpu.roll(here, nx - 1, 1))
                    near = near + (up + down) + (left + right)
                    centre = (6.0 - CENTRE) + diag[layer]
                    value = SCALE * (centre * here - near)
                    dst[v, shift + layer] = value
                    if j < 2:
                        stage_rows(j + 1, v, layer, value)
                return carry

            lax.fori_loop(ch * vc, (ch + 1) * vc, run, 0)
            if j < 2:
                @pl.when(below)
                def _():
                    z_copy(j + 1, ch, 0).start()

                @pl.when(above)
                def _():
                    z_copy(j + 1, ch, 1).start()

                start_rows(j + 1, ch)
            if j == 0:
                for layer in range(lay // 2):
                    back_copy(1, ch, layer).start()
            elif j == 1:
                for layer in range(lay // 2, lay):
                    back_copy(1, ch, layer).start()
            else:
                for layer in range(lay):
                    back_copy(2, ch, layer).start()

        chunks(apply)
        gram(2 * j + 1, src, dst, 1, shift, group_lay, half)
        gram(2 * j + 2, dst, dst, shift, shift, group_lay, half)

    for j in range(ITERS):
        step(j)

    count = acc.shape[0]
    sums = nt_dot(jnp.ones((8, 128), jnp.float32), acc[...])
    lane_q = lax.broadcasted_iota(jnp.int32, (8, count), 1)
    row_q = lax.broadcasted_iota(jnp.int32, (8, count), 0)
    q = lax.broadcasted_iota(jnp.int32, (count, 128), 0)
    c = lax.broadcasted_iota(jnp.int32, (count, 128), 1)
    pick = (q // (blk * blk) == c // blk) & (q % blk == c % blk)
    kept = jnp.where((lane_q // blk) % blk == row_q, sums, 0.0)
    local = dot(kept, jnp.where(pick, 1.0, 0.0))
    mine[...] = local
    slots1[gy] = local

    def along(n, me, src, slots, send, recv, axis):
        at = (lambda i: (gz, i)) if axis == "gy" else (lambda i: (i, gy))
        for off in range(1, n):
            to = (me + off) % n
            remote(src, slots.at[me], send.at[to], recv.at[me], at(to)).start()
        for off in range(1, n):
            frm = (me + off) % n
            remote(src, slots.at[frm], send.at[frm], recv.at[frm], at(frm)).wait()
        total = slots[0]
        for i in range(1, n):
            total = total + slots[i]
        return total

    summed = along(n_y, gy, mine, slots1, g1_s, g1_r, "gy")
    part[...] = summed
    slots2[gz] = summed
    moments = along(n_z, gz, part, slots2, g2_s, g2_r, "gz")

    lane = lax.broadcasted_iota(jnp.int32, (8, 128), 1)
    keep = lambda x, low, high: jnp.where((lane >= low) & (lane < high), x, 0.0)
    left_by = lambda x, n: x if n == 0 else pltpu.roll(x, 128 - n, 1)
    order = (ITERS + 1) * blk
    lane32 = lax.broadcasted_iota(jnp.int32, (order, 128), 1)
    row32 = lax.broadcasted_iota(jnp.int32, (order, 128), 0)
    full = jnp.concatenate(
        [keep(left_by(moments, blk * i), 0, order) for i in range(ITERS + 1)], axis=0
    )
    full = full + jnp.where(lane32 == row32 + order, 1.0, 0.0)
    inv = 1.0 / SCALE
    second = (
        (inv * inv) * left_by(moments, 2 * blk)
        + (2.0 * CENTRE * inv) * left_by(moments, blk)
        + (CENTRE * CENTRE) * moments
    )
    target = inv * left_by(moments, blk) + CENTRE * moments
    small = ITERS * blk
    normal = jnp.concatenate(
        [
            keep(left_by(second, blk * i), 0, small)
            + keep(pltpu.roll(target, small - blk * i, 1) if i < ITERS else target, small, order)
            for i in range(ITERS)
        ],
        axis=0,
    )
    rows_small = lax.broadcasted_iota(jnp.int32, (small, 1), 0)
    rows_full = lax.broadcasted_iota(jnp.int32, (order, 1), 0)
    for k in range(order):
        if k < small:
            row = normal[k:k + 1] / normal[k:k + 1, k:k + 1]
            column = jnp.where(rows_small == k, 0.0, normal[:, k:k + 1])
            normal = jnp.where(rows_small == k, row, normal - column * row)
        row = full[k:k + 1] / full[k:k + 1, k:k + 1]
        column = jnp.where(rows_full <= k, 0.0, full[:, k:k + 1])
        full = full - column * row
    pivots = jnp.sum(jnp.where(lane32 == row32, full, 0.0), axis=1, keepdims=True)
    full = full / jnp.sqrt(pivots)
    upper = jnp.where((lane32 < order) & (lane32 >= row32), full, 0.0)
    lower_inv = left_by(full, order)
    lower_inv = jnp.where(lane32 < small, lower_inv, 0.0)[:small]
    hess = inv * nt_dot(pltpu.roll(lower_inv, blk, 1), upper)
    eye = lax.broadcasted_iota(jnp.int32, (small, order), 0) == lax.broadcasted_iota(
        jnp.int32, (small, order), 1
    )
    row_b = lax.broadcasted_iota(jnp.int32, (small, order), 0) // blk
    col_b = lax.broadcasted_iota(jnp.int32, (small, order), 1) // blk
    hess = hess + jnp.where(eye, CENTRE, 0.0)
    hess_ref[...] = jnp.where(col_b <= row_b + 1, hess, 0.0)

    for k in range(small):
        for u in range(blk):
            splat[k * blk + u] = jnp.broadcast_to(
                normal[k:k + 1, small + u:small + u + 1], (8, 128)
            )

    def combine(dst, layers, row_start, height, sources):
        tiles = height // 8

        def run(i, carry):
            layer, t = layers[0] + i // tiles, i % tiles
            at = pl.multiple_of(row_start + t * 8, 8)
            for lane_at in range(lanes):
                cols = pl.ds(lane_at * 128, 128)
                vals = []
                for ref, l_at, base in sources:
                    first_row = pl.multiple_of(base + t * 8, 8)
                    vals += [ref[v, l_at + layer, pl.ds(first_row, 8), cols] for v in range(blk)]
                for u in range(blk):
                    total = splat[u] * vals[0]
                    for k in range(1, small):
                        total = total + splat[k * blk + u] * vals[k]
                    dst[u, layer, pl.ds(at, 8), cols] = total
            return carry

        lax.fori_loop(0, (layers[1] - layers[0]) * tiles, run, 0)

    for layer in range(lay):
        combine(held, (layer, layer + 1), 0, late, [(k, 1 + theirs_at, early) for k in basis[:ITERS]])
        late_copy(layer).start()
    combine(
        out_ref, (0, lay), hs, half, ((r_ref, 0, hs), (k1, 1 + mine_at, 0), (k2, 1 + mine_at, 0))
    )

    def back_wait(ch):
        for j in (1, 2):
            for layer in range(lay):
                back_copy(j, ch, layer).wait()

    chunks(back_wait)
    combine(out_ref, (0, lay), os, early, ((r_ref, 0, os), (ret1, 0, 0), (ret2, 0, 0)))
    for layer in range(lay):
        late_copy(layer).wait_send()
        remote(
            held.at[:, pl.ds(layer, 1)],
            out_ref.at[:, pl.ds(layer, 1), pl.ds(pl.multiple_of(os + early, 8), late)],
            l_s.at[layer], l_r.at[layer], (partner, gy),
        ).wait_recv()

    def drain(ch):
        for which in (0, 1):
            exchange(which, ch).wait_send()
        for j in range(ITERS):
            @pl.when(below)
            def _():
                z_copy(j, ch, 0).wait_send()

            @pl.when(above)
            def _():
                z_copy(j, ch, 1).wait_send()

            @pl.when(before)
            def _():
                y_copy(j, ch, 0).wait_send()

            @pl.when(after)
            def _():
                y_copy(j, ch, 1).wait_send()

    chunks(drain)
    diag_copy.wait_send()


def body(right_side, diagonal):
    blk, lay, rows, nx = right_side.shape
    half, group_lay = rows // 2, 2 * lay
    early = half * EARLY // 32 * 8
    n_z, n_y = lax.axis_size("gz"), lax.axis_size("gy")
    vmem = lambda *shape: pltpu.VMEM(shape, jnp.float32)
    dma = lambda *shape: pltpu.SemaphoreType.DMA(shape)
    small, order = ITERS * blk, (ITERS + 1) * blk
    return pl.pallas_call(
        kernel,
        out_shape=(
            jax.ShapeDtypeStruct(right_side.shape, jnp.float32),
            jax.ShapeDtypeStruct((small, order), jnp.float32),
        ),
        in_specs=[pl.BlockSpec(memory_space=pltpu.VMEM)] * 2,
        out_specs=(pl.BlockSpec(memory_space=pltpu.VMEM),) * 2,
        scratch_shapes=[
            vmem(blk, group_lay + 2, half, nx),
            vmem(blk, group_lay + 2, half, nx),
            vmem(blk, group_lay + 2, half, nx),
            vmem(blk, group_lay, half, nx),
            vmem(group_lay, half, nx),
            vmem(blk, lay, early, nx),
            vmem(blk, lay, early, nx),
            vmem(blk, lay, half - early, nx),
            vmem(ITERS, 2, blk, group_lay, nx),
            vmem(ITERS, 2, blk, group_lay, nx),
            vmem(8 * blk * blk, 128),
            vmem(8, 128),
            vmem(n_y, 8, 128),
            vmem(8, 128),
            vmem(n_z, 8, 128),
            vmem(small * blk, 8, 128),
            dma(2, CHUNKS), dma(2, CHUNKS),
            pltpu.SemaphoreType.DMA, pltpu.SemaphoreType.DMA,
            dma(ITERS, 2, CHUNKS), dma(ITERS, 2, CHUNKS),
            dma(ITERS, 2, CHUNKS), dma(ITERS, 2, CHUNKS),
            dma(2, lay, CHUNKS), dma(2, lay, CHUNKS), dma(lay), dma(lay),
            dma(n_y), dma(n_y), dma(n_z), dma(n_z),
        ],
        compiler_params=pltpu.CompilerParams(
            collective_id=0, has_side_effects=True, vmem_limit_bytes=60 * 1024 * 1024
        ),
        name="gmres",
    )(right_side, diagonal)


def solution(mesh):
    in_specs = (P(None, "gz", "gy", None), P("gz", "gy", None))
    out_specs = (P(None, "gz", "gy", None), P())
    return jax.shard_map(body, mesh=mesh, in_specs=in_specs, out_specs=out_specs, check_vma=False)
```

profile of v0, /device:TPU:0, one launch (start us, length us, event | category | flops | bytes accessed | tf_op | source)
XLA Modules:
  0.0 89.2 jit_solution(3501788388570530835)
XLA Ops:
  0.6 84.8 %gmres.1 = (f32[8,2,64,512]{3,2,1,0:T(8,128)}, f32[24,32]{1,0:T(8,128)}) custom-call(f32[8,2,64,512]{3,2,1,0:T(8,128)} %r_ref.1, f32[2,64,512]{2,1,0:T(8,128)} %d_ref.1), custom_call_target="tpu_custom_call" | custom-call | tf_op jit(solution)/shard_map/gmres/pallas_call | solution.py:508
  85.5 0.0 copy-start
  85.5 3.1 %copy.6 = f32[8,2,64,512]{3,2,1,0:T(8,128)} copy(f32[8,2,64,512]{3,2,1,0:T(8,128)} %get-tuple-element.4) | data formatting | bytes 4194304
  88.6 0.0 copy-done
  88.6 0.6 copy.7
Async XLA Ops:
  85.5 3.2 %copy-start = (f32[24,32]{1,0:T(8,128)S(1)}, f32[24,32]{1,0:T(8,128)}, u32[]{:S(2)}) copy-start(f32[24,32]{1,0:T(8,128)} %get-tuple-element.5) | copy-start | bytes 9220
where the time goes:
time: 89.4 us; the launch traced here: 89.2 us
  Pallas kernels  84.8 us (95%)
  local copies, waits for them, and re-layouts  3.75 us (4%)
    pallas_call x1, Pallas kernels, body(): pl.pallas_call(kernel, out_shape=(jax.ShapeDtypeStruct(right_side.shape,...  84.8 us
    unnamed x4, local copies, waits for them, and re-layouts  3.75 us

commit v1 on v0

v1 whole, which is shorter than its diff:
```python
import functools

import jax
import jax.numpy as jnp
from jax import lax
from jax.experimental import pallas as pl
from jax.experimental.pallas import tpu as pltpu
from jax.sharding import PartitionSpec as P

ITERS = 3
CENTRE = 7.5
SCALE = 0.25
CHUNKS = 4
EARLY = 2
BACK = {
    (0, 3): ((1, 0), (1, 1)), (1, 0): ((1, 2),), (1, 1): ((1, 3),), (1, 2): ((2, 0),),
    (1, 3): ((2, 1),), (2, 0): ((2, 2),), "reduce": ((2, 3),),
}
MESH = pl.DeviceIdType.MESH
HIGH = lax.Precision.HIGHEST


def SC(name, f):
    with jax.named_scope(name):
        return f()


def nt_dot(left, right):
    return lax.dot_general(
        left, right, (((1,), (1,)), ((), ())), precision=HIGH, preferred_element_type=jnp.float32
    )


def dot(left, right):
    return jnp.dot(left, right, precision=HIGH, preferred_element_type=jnp.float32)


def kernel(
    r_hbm, d_hbm, out_ref, hess_ref,
    r_ref, d_ref, k0, k1, k2, k3, diag, ret1, ret2, held, ys, yh, rows_out, rows_in,
    acc, mine, slots, splat, i_s,
    x_s, x_r, d_s, d_r, z_s, z_r, y_s, y_r, e_s, e_r, b_s, b_r, l_s, l_r, g_s, g_r,
):
    blk, lay, rows, nx = r_ref.shape
    half, group_lay = rows // 2, 2 * lay
    vc = blk // CHUNKS
    n_z, n_y = lax.axis_size("gz"), lax.axis_size("gy")
    gz, gy = lax.axis_index("gz"), lax.axis_index("gy")
    n_dev = n_z * n_y
    me = gz * n_y + gy
    p, group = gz % 2, gz // 2
    h = (p + gy) % 2
    partner = gz + 1 - 2 * p
    hs = pl.multiple_of(h * half, half)
    os = pl.multiple_of((1 - h) * half, half)
    mine_at = p * lay
    theirs_at = (1 - p) * lay
    below, above = group > 0, group < n_z // 2 - 1
    place = 2 * gy + h
    before, after = place > 0, place < 2 * n_y - 1
    prev_dev = (gz + h * (partner - gz), gy - (1 - h))
    next_dev = (gz + (1 - h) * (partner - gz), gy + h)
    basis = (k0, k1, k2, k3)
    edge = (lay - 1) * p

    def remote(src, dst, send, recv, dev):
        return pltpu.make_async_remote_copy(
            src_ref=src, dst_ref=dst, send_sem=send, recv_sem=recv, device_id=dev,
            device_id_type=MESH,
        )

    def device(i):
        return (i // n_y, i % n_y)

    load_r = pltpu.make_async_copy(r_hbm, r_ref, i_s.at[0])
    load_d = pltpu.make_async_copy(d_hbm, d_ref, i_s.at[1])
    load_r.start()
    load_d.start()

    barrier = pltpu.get_barrier_semaphore()

    def greet(off, carry):
        pl.semaphore_signal(
            barrier, inc=1, device_id=device((me + off) % n_dev), device_id_type=MESH
        )
        return carry

    lax.fori_loop(1, n_dev, greet, 0)

    @pl.when(jnp.logical_not(below))
    def _():
        for k in (k0, k1, k2):
            k[:, 0] = jnp.zeros((blk, half, nx), jnp.float32)

    @pl.when(jnp.logical_not(above))
    def _():
        for k in (k0, k1, k2):
            k[:, group_lay + 1] = jnp.zeros((blk, half, nx), jnp.float32)

    @pl.when(jnp.logical_not(before))
    def _():
        yh[:, 0] = jnp.zeros((ITERS,) + yh.shape[2:], jnp.float32)

    @pl.when(jnp.logical_not(after))
    def _():
        yh[:, 1] = jnp.zeros((ITERS,) + yh.shape[2:], jnp.float32)

    load_r.wait()
    for v in range(blk):
        rows_out[v] = jnp.where(
            h == 0, r_ref[v, :, half - 1:half], r_ref[v, :, half:half + 1]
        )
    SC("barrier", lambda: pl.semaphore_wait(barrier, n_dev - 1))

    rows_copy = remote(rows_out, rows_in, e_s, e_r, (partner, gy))
    rows_copy.start()

    def exchange(which, ch):
        layer = edge + which * (1 - 2 * p)
        vs = pl.ds(ch * vc, vc)
        return remote(
            r_ref.at[vs, pl.ds(layer, 1), pl.ds(os, half)],
            k0.at[vs, pl.ds(1 + mine_at + layer, 1)],
            x_s.at[which, ch], x_r.at[which, ch], (partner, gy),
        )

    def z_from_rhs(ch, direction):
        vs = pl.ds(ch * vc, vc)
        if direction == 0:
            dst, dev = k0.at[vs, pl.ds(group_lay + 1, 1)], (gz - 2, gy)
        else:
            dst, dev = k0.at[vs, pl.ds(0, 1)], (gz + 2, gy)
        return remote(
            r_ref.at[vs, pl.ds(edge, 1), pl.ds(hs, half)], dst,
            z_s.at[0, direction, ch], z_r.at[0, direction, ch], dev,
        )

    def z_copy(j, ch, direction):
        vs = pl.ds(ch * vc, vc)
        k = basis[j]
        if direction == 0:
            src, dst, dev = k.at[vs, pl.ds(1, 1)], k.at[vs, pl.ds(group_lay + 1, 1)], (gz - 2, gy)
        else:
            src, dst, dev = k.at[vs, pl.ds(group_lay, 1)], k.at[vs, pl.ds(0, 1)], (gz + 2, gy)
        return remote(src, dst, z_s.at[j, direction, ch], z_r.at[j, direction, ch], dev)

    def y_copy(j, ch, side):
        vs = pl.ds(ch * vc, vc)
        dev = prev_dev if side == 0 else next_dev
        return remote(
            ys.at[j, side, vs], yh.at[j, 1 - side, vs],
            y_s.at[j, side, ch], y_r.at[j, 1 - side, ch], dev,
        )

    def y_wait_recv(j, ch, side):
        vs = pl.ds(ch * vc, vc)
        remote(
            ys.at[j, side, vs], yh.at[j, side, vs], y_s.at[j, side, ch], y_r.at[j, side, ch],
            (partner, gy),
        ).wait_recv()

    def has(j, side):
        if side == 0:
            return before if j else before & (h == 0)
        return after if j else after & (h == 1)

    early = ret1.shape[2]
    late = half - early

    def back_copy(j, ch):
        vs = pl.ds(ch * vc, vc)
        dst = (ret1, ret2)[j - 1]
        return remote(
            basis[j].at[vs, pl.ds(1 + theirs_at, lay), pl.ds(0, early)],
            dst.at[vs], b_s.at[j - 1, ch], b_r.at[j - 1, ch], (partner, gy),
        )

    def late_copy(layer):
        return remote(
            held.at[:, pl.ds(layer, 1)],
            out_ref.at[:, pl.ds(layer, 1), pl.ds(pl.multiple_of(hs + early, 8), late)],
            l_s.at[layer], l_r.at[layer], (partner, gy),
        )

    diag_copy = remote(
        d_ref.at[:, pl.ds(os, half)], diag.at[pl.ds(mine_at, lay)], d_s, d_r, (partner, gy)
    )

    for ch in range(CHUNKS):
        exchange(0, ch).start()

        @pl.when((p == 0) & below)
        def _():
            z_from_rhs(ch, 0).start()

        @pl.when((p == 1) & above)
        def _():
            z_from_rhs(ch, 1).start()

    load_d.wait()
    diag_copy.start()
    for ch in range(CHUNKS):
        exchange(1, ch).start()

    def own(v, carry):
        k0[v, pl.ds(1 + mine_at, lay)] = r_ref[v, :, pl.ds(hs, half)]
        return carry

    lax.fori_loop(0, blk, own, 0)
    diag[pl.ds(mine_at, lay)] = d_ref[:, pl.ds(hs, half)]

    lanes = nx // 128

    def add_up(sums, tiles):
        def run(i, carry):
            layer, at = i // tiles, pl.multiple_of((i % tiles) * 8, 8)
            for lane in range(lanes):
                carry = sums(carry, layer, at, pl.ds(lane * 128, 128))
            return carry
        return run

    def keep_sum(moment, a, b, s):
        line = jnp.sum(s, axis=0, keepdims=True)
        at = (moment * blk + a) * blk + b
        acc[at:at + 1] = line
        if a != b:
            at = (moment * blk + b) * blk + a
            acc[at:at + 1] = line

    zero = jnp.zeros((8, 128), jnp.float32)

    def gram_rhs():
        pairs = [(a, b) for a in range(blk) for b in range(a, blk)]

        def body(sums, layer, at, cols):
            x = [r_ref[v, layer, pl.ds(at, 8), cols] for v in range(blk)]
            return tuple(s + x[a] * x[b] for s, (a, b) in zip(sums, pairs))

        sums = lax.fori_loop(
            0, lay * (rows // 8), add_up(body, rows // 8), (zero,) * len(pairs)
        )
        for s, (a, b) in zip(sums, pairs):
            keep_sum(0, a, b, s)

    def gram(j, ch):
        src, dst = basis[j], basis[j + 1]
        shift = 0 if j == ITERS - 1 else 1
        top = (ch + 1) * vc
        pairs = [(a, b) for b in range(ch * vc, top) for a in range(b + 1)]

        def body(sums, layer, at, cols):
            x = [src[v, 1 + layer, pl.ds(at, 8), cols] for v in range(top)]
            y = [dst[v, shift + layer, pl.ds(at, 8), cols] for v in range(top)]
            first, second = sums[:len(pairs)], sums[len(pairs):]
            first = tuple(s + x[a] * y[b] for s, (a, b) in zip(first, pairs))
            second = tuple(s + y[a] * y[b] for s, (a, b) in zip(second, pairs))
            return first + second

        sums = lax.fori_loop(
            0, group_lay * (half // 8), add_up(body, half // 8), (zero,) * (2 * len(pairs))
        )
        for i, (a, b) in enumerate(pairs):
            keep_sum(2 * j + 1, a, b, sums[i])
            keep_sum(2 * j + 2, a, b, sums[len(pairs) + i])

    acc[7 * blk * blk:] = jnp.zeros((acc.shape[0] - 7 * blk * blk, 128), jnp.float32)
    SC("gram0", gram_rhs)

    def relay(ch):
        remote(
            r_ref.at[pl.ds(0, vc), pl.ds(0, 1), pl.ds(os, half)],
            k0.at[pl.ds(ch * vc, vc), pl.ds(1 + (group_lay - 1) * (1 - p), 1)],
            x_s.at[0, ch], x_r.at[0, ch], (partner, gy),
        ).wait_recv()

        @pl.when((p == 0) & above)
        def _():
            z_copy(0, ch, 1).start()

        @pl.when((p == 1) & below)
        def _():
            z_copy(0, ch, 0).start()

    def stage_rows(j, v, layer, value):
        ys[j, 0, v, layer:layer + 1] = value[:1]
        ys[j, 1, v, layer:layer + 1] = value[half - 1:]

    def start_rows(j, ch):
        for side in range(2):
            @pl.when(has(j, side))
            def _():
                y_copy(j, ch, side).start()

    def arrived(ch):
        remote(
            r_ref.at[pl.ds(0, vc), pl.ds(0, 1), pl.ds(os, half)],
            k0.at[pl.ds(ch * vc, vc), pl.ds(1 + lay - p, 1)],
            x_s.at[1, ch], x_r.at[1, ch], (partner, gy),
        ).wait_recv()

        def run(v, carry):
            for layer in range(group_lay):
                stage_rows(0, v, layer, k0[v, 1 + layer])
            return carry

        lax.fori_loop(ch * vc, (ch + 1) * vc, run, 0)
        start_rows(0, ch)

    for ch in range(CHUNKS):
        SC(f"relay#{ch}", lambda: relay(ch))

    def rows_arrived():
        rows_copy.wait()
        for v in range(blk):
            near = jnp.where(
                h == 0, r_ref[v, :, half:half + 1], r_ref[v, :, half - 1:half]
            ).reshape(lay, nx)
            far = rows_in[v].reshape(lay, nx)
            yh[0, 1 - h, v] = jnp.where(
                p == 0,
                jnp.concatenate([near, far], axis=0),
                jnp.concatenate([far, near], axis=0),
            )
        remote(
            d_ref.at[:, pl.ds(os, half)], diag.at[pl.ds(theirs_at, lay)], d_s, d_r, (partner, gy)
        ).wait_recv()

    SC("rows_diag", rows_arrived)

    row_at = lax.broadcasted_iota(jnp.int32, (half, nx), 0)
    col_at = lax.broadcasted_iota(jnp.int32, (half, nx), 1)

    def apply(j, ch):
        src, dst = basis[j], basis[j + 1]
        shift = 0 if j == ITERS - 1 else 1
        vs = pl.ds(ch * vc, vc)

        def waits():
            @pl.when(below)
            def _():
                remote(
                    src.at[vs, pl.ds(1, 1)], src.at[vs, pl.ds(0, 1)],
                    z_s.at[j, 1, ch], z_r.at[j, 1, ch], (partner, gy),
                ).wait_recv()

            @pl.when(above)
            def _():
                remote(
                    src.at[vs, pl.ds(1, 1)], src.at[vs, pl.ds(group_lay + 1, 1)],
                    z_s.at[j, 0, ch], z_r.at[j, 0, ch], (partner, gy),
                ).wait_recv()

        def row_waits():
            for side in range(2):
                @pl.when(has(j, side))
                def _():
                    y_wait_recv(j, ch, side)

        SC(f"z_wait{j}#{ch}", waits)
        SC(f"y_wait{j}#{ch}", row_waits)

        def run(v, carry):
            for layer in range(group_lay):
                here = src[v, 1 + layer]
                near = src[v, layer] + src[v, 2 + layer]
                up = jnp.where(
                    row_at == 0, yh[j, 0, v, layer:layer + 1], pltpu.roll(here, 1, 0)
                )
                down = jnp.where(
                    row_at == half - 1, yh[j, 1, v, layer:layer + 1],
                    pltpu.roll(here, half - 1, 0),
                )
                left = jnp.where(col_at == 0, 0.0, pltpu.roll(here, 1, 1))
                right = jnp.where(col_at == nx - 1, 0.0, pltpu.roll(here, nx - 1, 1))
                near = near + (up + down) + (left + right)
                centre = (6.0 - CENTRE) + diag[layer]
                value = SCALE * (centre * here - near)
                dst[v, shift + layer] = value
                if j < ITERS - 1:
                    stage_rows(j + 1, v, layer, value)
            return carry

        SC(f"apply{j}#{ch}", lambda: lax.fori_loop(ch * vc, (ch + 1) * vc, run, 0))
        if j < ITERS - 1:
            @pl.when(below)
            def _():
                z_copy(j + 1, ch, 0).start()

            @pl.when(above)
            def _():
                z_copy(j + 1, ch, 1).start()

            start_rows(j + 1, ch)
        for item in BACK.get((j, ch), ()):
            back_copy(*item).start()
        SC(f"gram{j}#{ch}", lambda: gram(j, ch))

    for ch in range(CHUNKS):
        SC(f"arrived#{ch}", lambda: arrived(ch))
        apply(0, ch)
    for j in range(1, ITERS):
        for ch in range(CHUNKS):
            apply(j, ch)

    def reduce():
        count = acc.shape[0]
        sums = nt_dot(jnp.ones((8, 128), jnp.float32), acc[...])
        lane_q = lax.broadcasted_iota(jnp.int32, (8, count), 1)
        row_q = lax.broadcasted_iota(jnp.int32, (8, count), 0)
        q = lax.broadcasted_iota(jnp.int32, (count, 128), 0)
        c = lax.broadcasted_iota(jnp.int32, (count, 128), 1)
        pick = (q // (blk * blk) == c // blk) & (q % blk == c % blk)
        kept = jnp.where((lane_q // blk) % blk == row_q, sums, 0.0)
        local = dot(kept, jnp.where(pick, 1.0, 0.0))
        packed = local[:4] + pltpu.roll(local, 64, 1)[4:]
        mine[...] = packed
        slots[me] = packed

        def send(off, carry):
            to = (me + off) % n_dev
            remote(mine, slots.at[me], g_s.at[to], g_r.at[me], device(to)).start()
            return carry

        lax.fori_loop(1, n_dev, send, 0)
        for item in BACK.get("reduce", ()):
            back_copy(*item).start()

    SC("red_send", reduce)

    def collect():
        def take(off, carry):
            frm = (me + off) % n_dev
            remote(mine, slots.at[frm], g_s.at[frm], g_r.at[frm], device(frm)).wait()
            return carry

        lax.fori_loop(1, n_dev, take, 0)

    SC("red_wait", collect)
    packed = jnp.sum(slots[...], axis=0)

    lane = lax.broadcasted_iota(jnp.int32, (8, 128), 1)
    keep = lambda x, low, high: jnp.where((lane >= low) & (lane < high), x, 0.0)
    left_by = lambda x, n: x if n == 0 else pltpu.roll(x, 128 - n, 1)
    moments = keep(
        jnp.concatenate([packed, pltpu.roll(packed, 64, 1)], axis=0), 0, 64
    )
    def solve():
        order = (ITERS + 1) * blk
        lane32 = lax.broadcasted_iota(jnp.int32, (order, 128), 1)
        row32 = lax.broadcasted_iota(jnp.int32, (order, 128), 0)
        full = jnp.concatenate(
            [keep(left_by(moments, blk * i), 0, order) for i in range(ITERS + 1)], axis=0
        )
        full = full + jnp.where(lane32 == row32 + order, 1.0, 0.0)
        inv = 1.0 / SCALE
        second = (
            (inv * inv) * left_by(moments, 2 * blk)
            + (2.0 * CENTRE * inv) * left_by(moments, blk)
            + (CENTRE * CENTRE) * moments
        )
        target = inv * left_by(moments, blk) + CENTRE * moments
        small = ITERS * blk
        normal = jnp.concatenate(
            [
                keep(left_by(second, blk * i), 0, small)
                + keep(pltpu.roll(target, small - blk * i, 1) if i < ITERS else target, small, order)
                for i in range(ITERS)
            ],
            axis=0,
        )
        rows_small = lax.broadcasted_iota(jnp.int32, (small, 1), 0)
        rows_full = lax.broadcasted_iota(jnp.int32, (order, 1), 0)
        for k in range(order):
            if k < small:
                row = normal[k:k + 1] / normal[k:k + 1, k:k + 1]
                column = jnp.where(rows_small == k, 0.0, normal[:, k:k + 1])
                normal = jnp.where(rows_small == k, row, normal - column * row)
            row = full[k:k + 1] / full[k:k + 1, k:k + 1]
            column = jnp.where(rows_full <= k, 0.0, full[:, k:k + 1])
            full = full - column * row
        pivots = jnp.sum(jnp.where(lane32 == row32, full, 0.0), axis=1, keepdims=True)
        full = full / jnp.sqrt(pivots)
        upper = jnp.where((lane32 < order) & (lane32 >= row32), full, 0.0)
        lower_inv = left_by(full, order)
        lower_inv = jnp.where(lane32 < small, lower_inv, 0.0)[:small]
        hess = inv * nt_dot(pltpu.roll(lower_inv, blk, 1), upper)
        eye = lax.broadcasted_iota(jnp.int32, (small, order), 0) == lax.broadcasted_iota(
            jnp.int32, (small, order), 1
        )
        row_b = lax.broadcasted_iota(jnp.int32, (small, order), 0) // blk
        col_b = lax.broadcasted_iota(jnp.int32, (small, order), 1) // blk
        hess = hess + jnp.where(eye, CENTRE, 0.0)
        hess_ref[...] = jnp.where(col_b <= row_b + 1, hess, 0.0)
        return normal

    normal = SC("solve", solve)
    small = ITERS * blk

    def spread():
        for k in range(small):
            for u in range(blk):
                splat[k * blk + u] = jnp.broadcast_to(
                    normal[k:k + 1, small + u:small + u + 1], (8, 128)
                )

    SC("splat", spread)

    def combine(dst, layers, row_start, height, sources):
        tiles = height // 8

        def run(i, carry):
            layer, t = layers[0] + i // tiles, i % tiles
            at = pl.multiple_of(row_start + t * 8, 8)
            for lane_at in range(lanes):
                cols = pl.ds(lane_at * 128, 128)
                vals = []
                for ref, l_at, base in sources:
                    first_row = pl.multiple_of(base + t * 8, 8)
                    vals += [ref[v, l_at + layer, pl.ds(first_row, 8), cols] for v in range(blk)]
                for u in range(blk):
                    total = splat[u] * vals[0]
                    for k in range(1, small):
                        total = total + splat[k * blk + u] * vals[k]
                    dst[u, layer, pl.ds(at, 8), cols] = total
            return carry

        lax.fori_loop(0, (layers[1] - layers[0]) * tiles, run, 0)

    def send_late():
        for layer in range(lay):
            combine(held, (layer, layer + 1), 0, late, [(k, 1 + theirs_at, early) for k in basis[:ITERS]])
            late_copy(layer).start()

    SC("comb_late", send_late)
    SC("comb_own", lambda: combine(
        out_ref, (0, lay), hs, half, ((r_ref, 0, hs), (k1, 1 + mine_at, 0), (k2, 1 + mine_at, 0))
    ))

    def back_wait():
        for j in (1, 2):
            for ch in range(CHUNKS):
                back_copy(j, ch).wait()

    SC("back_wait", back_wait)
    SC("comb_other", lambda: combine(
        out_ref, (0, lay), os, early, ((r_ref, 0, os), (ret1, 0, 0), (ret2, 0, 0))
    ))

    def late_wait():
        for layer in range(lay):
            late_copy(layer).wait_send()
            remote(
                held.at[:, pl.ds(layer, 1)],
                out_ref.at[:, pl.ds(layer, 1), pl.ds(pl.multiple_of(os + early, 8), late)],
                l_s.at[layer], l_r.at[layer], (partner, gy),
            ).wait_recv()

    SC("late_wait", late_wait)

    for ch in range(CHUNKS):
        for which in (0, 1):
            exchange(which, ch).wait_send()

        @pl.when(below)
        def _():
            z_copy(0, ch, 0).wait_send()

        @pl.when(above)
        def _():
            z_copy(0, ch, 1).wait_send()

        for j in range(1, ITERS):
            @pl.when(below)
            def _():
                z_copy(j, ch, 0).wait_send()

            @pl.when(above)
            def _():
                z_copy(j, ch, 1).wait_send()

        for j in range(ITERS):
            for side in range(2):
                @pl.when(has(j, side))
                def _():
                    y_copy(j, ch, side).wait_send()

    diag_copy.wait_send()


def body(right_side, diagonal):
    blk, lay, rows, nx = right_side.shape
    half, group_lay = rows // 2, 2 * lay
    early = half * EARLY // 32 * 8
    n_z, n_y = lax.axis_size("gz"), lax.axis_size("gy")
    vmem = lambda *shape: pltpu.VMEM(shape, jnp.float32)
    dma = lambda *shape: pltpu.SemaphoreType.DMA(shape)
    small, order = ITERS * blk, (ITERS + 1) * blk
    in_hbm = lambda x: pltpu.with_memory_space_constraint(x, pltpu.HBM)
    return pl.pallas_call(
        kernel,
        out_shape=(vmem(*right_side.shape), vmem(small, order)),
        in_specs=[pl.BlockSpec(memory_space=pltpu.HBM)] * 2,
        out_specs=(pl.BlockSpec(memory_space=pltpu.VMEM),) * 2,
        scratch_shapes=[
            vmem(*right_side.shape),
            vmem(*diagonal.shape),
            vmem(blk, group_lay + 2, half, nx),
            vmem(blk, group_lay + 2, half, nx),
            vmem(blk, group_lay + 2, half, nx),
            vmem(blk, group_lay, half, nx),
            vmem(group_lay, half, nx),
            vmem(blk, lay, early, nx),
            vmem(blk, lay, early, nx),
            vmem(blk, lay, half - early, nx),
            vmem(ITERS, 2, blk, group_lay, nx),
            vmem(ITERS, 2, blk, group_lay, nx),
            vmem(blk, lay, 1, nx),
            vmem(blk, lay, 1, nx),
            vmem(8 * blk * blk, 128),
            vmem(4, 128),
            vmem(n_z * n_y, 4, 128),
            vmem(small * blk, 8, 128),
            dma(2),
            dma(2, CHUNKS), dma(2, CHUNKS),
            pltpu.SemaphoreType.DMA, pltpu.SemaphoreType.DMA,
            dma(ITERS, 2, CHUNKS), dma(ITERS, 2, CHUNKS),
            dma(ITERS, 2, CHUNKS), dma(ITERS, 2, CHUNKS),
            pltpu.SemaphoreType.DMA, pltpu.SemaphoreType.DMA,
            dma(2, CHUNKS), dma(2, CHUNKS), dma(lay), dma(lay),
            dma(n_z * n_y), dma(n_z * n_y),
        ],
        compiler_params=pltpu.CompilerParams(
            collective_id=0, has_side_effects=True, vmem_limit_bytes=40 * 1024 * 1024
        ),
        name="gmres",
    )(in_hbm(right_side), in_hbm(diagonal))


def solution(mesh):
    in_specs = (P(None, "gz", "gy", None), P("gz", "gy", None))
    out_specs = (P(None, "gz", "gy", None), P())
    return jax.shard_map(body, mesh=mesh, in_specs=in_specs, out_specs=out_specs, check_vma=False)
```

time: 89.4 us -> 83.1 us (0.930)
  Pallas kernels: 84.8 us -> 80.4 us
  local copies, waits for them, and re-layouts: 3.75 us -> 1.92 us
    pallas_call x1, Pallas kernels: 84.8 us -> 80.4 us  [body(): pl.pallas_call(kernel, out_shape=(vmem(*right_side.shape), vmem(small, or...]
    unnamed x4 -> x2, local copies, waits for them, and re-layouts: 3.75 us -> 1.92 us
where the time goes in v1:
time: 83.1 us; the launch traced here: 82.9 us
  Pallas kernels  80.4 us (97%)
  local copies, waits for them, and re-layouts  1.92 us (2%)
    pallas_call x1, Pallas kernels, body(): pl.pallas_call(kernel, out_shape=(vmem(*right_side.shape), vmem(small, or...  80.4 us
    unnamed x2, local copies, waits for them, and re-layouts  1.92 us

profile of v1, /device:TPU:0, one launch (start us, length us, event | category | flops | bytes accessed | tf_op | source)
XLA Modules:
  0.0 82.9 jit_solution(2297339204073631143)
XLA Ops:
  0.6 80.4 %gmres.1 = (f32[8,2,64,512]{3,2,1,0:T(8,128)S(1)}, f32[24,32]{1,0:T(8,128)S(1)}) custom-call(f32[8,2,64,512]{3,2,1,0:T(8,128)} %r_hbm.1, f32[2,64,512]{2,1,0:T(8,128)} %d_hbm.1), custom_call_target="tpu_custom_call" | custom-call | tf_op jit(solution)/shard_map/gmres/pallas_call | solution.py:599
  81.0 1.3 %copy.6 = f32[8,2,64,512]{3,2,1,0:T(8,128)} copy(f32[8,2,64,512]{3,2,1,0:T(8,128)S(1)} %get-tuple-element.2) | data formatting | bytes 4194304
  82.3 0.6 copy.7

commit v2 on v1

--- a/solution.py
+++ b/solution.py
@@ -11,10 +11,12 @@
 CENTRE = 7.5
 SCALE = 0.25
 CHUNKS = 4
-EARLY = 2
+EARLY = (3, 2)
 BACK = {
-    (0, 3): ((1, 0), (1, 1)), (1, 0): ((1, 2),), (1, 1): ((1, 3),), (1, 2): ((2, 0),),
-    (1, 3): ((2, 1),), (2, 0): ((2, 2),), "reduce": ((2, 3),),
+    (0, 1): ((1, 0, 0),), (0, 2): ((1, 0, 1), (1, 1, 0)), (0, 3): ((1, 1, 1), (1, 2, 0)),
+    (1, 0): ((1, 2, 1),), (1, 2): ((1, 3, 0),), (1, 3): ((1, 3, 1),),
+    (2, 0): ((2, 0, 0), (2, 0, 1)), (2, 1): ((2, 1, 0),),
+    "reduce": ((2, 1, 1), (2, 2, 0), (2, 2, 1), (2, 3, 0), (2, 3, 1)),
 }
 MESH = pl.DeviceIdType.MESH
 HIGH = lax.Precision.HIGHEST
@@ -37,8 +39,8 @@
 
 def kernel(
     r_hbm, d_hbm, out_ref, hess_ref,
-    r_ref, d_ref, k0, k1, k2, k3, diag, ret1, ret2, held, ys, yh, rows_out, rows_in,
-    acc, mine, slots, splat, i_s,
+    r_ref, d_ref, k0, k1, k2, k3, diag, ret, held, ys, yh, rows_out, rows_in,
+    acc, mine, slots, splat, i_s, met,
     x_s, x_r, d_s, d_r, z_s, z_r, y_s, y_r, e_s, e_r, b_s, b_r, l_s, l_r, g_s, g_r,
 ):
     blk, lay, rows, nx = r_ref.shape
@@ -72,20 +74,39 @@
     def device(i):
         return (i // n_y, i % n_y)
 
-    load_r = pltpu.make_async_copy(r_hbm, r_ref, i_s.at[0])
-    load_d = pltpu.make_async_copy(d_hbm, d_ref, i_s.at[1])
-    load_r.start()
+    def load_r(ch):
+        vs = pl.ds(ch * vc, vc)
+        return pltpu.make_async_copy(r_hbm.at[vs], r_ref.at[vs], i_s.at[ch])
+
+    load_d = pltpu.make_async_copy(d_hbm, d_ref, i_s.at[CHUNKS])
+    for ch in range(CHUNKS):
+        load_r(ch).start()
     load_d.start()
 
+    def signal(semaphore, dev):
+        pl.semaphore_signal(semaphore, inc=1, device_id=dev, device_id_type=MESH)
+
     barrier = pltpu.get_barrier_semaphore()
-
-    def greet(off, carry):
-        pl.semaphore_signal(
-            barrier, inc=1, device_id=device((me + off) % n_dev), device_id_type=MESH
-        )
-        return carry
-
-    lax.fori_loop(1, n_dev, greet, 0)
+    left, right = gy > 0, gy < n_y - 1
+    sides = (
+        (below, (gz - 2, gy)), (above, (gz + 2, gy)), (left, (gz, gy - 1)), (right, (gz, gy + 1)),
+    )
+    signal(barrier, (partner, gy))
+    for there, dev in sides:
+        @pl.when(there)
+        def _():
+            signal(barrier, dev)
+
+    def wave(which):
+        there, back = sides[which], sides[which ^ 1]
+
+        @pl.when(back[0])
+        def _():
+            pl.semaphore_wait(met.at[which], 1)
+
+        @pl.when(there[0])
+        def _():
+            signal(met.at[which], there[1])
 
     @pl.when(jnp.logical_not(below))
     def _():
@@ -105,15 +126,11 @@
     def _():
         yh[:, 1] = jnp.zeros((ITERS,) + yh.shape[2:], jnp.float32)
 
-    load_r.wait()
-    for v in range(blk):
-        rows_out[v] = jnp.where(
-            h == 0, r_ref[v, :, half - 1:half], r_ref[v, :, half:half + 1]
-        )
-    SC("barrier", lambda: pl.semaphore_wait(barrier, n_dev - 1))
-
+    load_r(0).wait()
+    SC("barrier", lambda: pl.semaphore_wait(
+        barrier, 1 + sum(jnp.where(there, 1, 0) for there, _ in sides)
+    ))
     rows_copy = remote(rows_out, rows_in, e_s, e_r, (partner, gy))
-    rows_copy.start()
 
     def exchange(which, ch):
         layer = edge + which * (1 - 2 * p)
@@ -121,7 +138,7 @@
         return remote(
             r_ref.at[vs, pl.ds(layer, 1), pl.ds(os, half)],
             k0.at[vs, pl.ds(1 + mine_at + layer, 1)],
-            x_s.at[which, ch], x_r.at[which, ch], (partner, gy),
+            x_s, x_r.at[which, ch], (partner, gy),
         )
 
     def z_from_rhs(ch, direction):
@@ -132,7 +149,7 @@
             dst, dev = k0.at[vs, pl.ds(0, 1)], (gz + 2, gy)
         return remote(
             r_ref.at[vs, pl.ds(edge, 1), pl.ds(hs, half)], dst,
-            z_s.at[0, direction, ch], z_r.at[0, direction, ch], dev,
+            z_s.at[0, direction], z_r.at[0, direction, ch], dev,
         )
 
     def z_copy(j, ch, direction):
@@ -142,20 +159,20 @@
             src, dst, dev = k.at[vs, pl.ds(1, 1)], k.at[vs, pl.ds(group_lay + 1, 1)], (gz - 2, gy)
         else:
             src, dst, dev = k.at[vs, pl.ds(group_lay, 1)], k.at[vs, pl.ds(0, 1)], (gz + 2, gy)
-        return remote(src, dst, z_s.at[j, direction, ch], z_r.at[j, direction, ch], dev)
+        return remote(src, dst, z_s.at[j, direction], z_r.at[j, direction, ch], dev)
 
     def y_copy(j, ch, side):
         vs = pl.ds(ch * vc, vc)
         dev = prev_dev if side == 0 else next_dev
         return remote(
             ys.at[j, side, vs], yh.at[j, 1 - side, vs],
-            y_s.at[j, side, ch], y_r.at[j, 1 - side, ch], dev,
+            y_s.at[j, side], y_r.at[j, 1 - side, ch], dev,
         )
 
     def y_wait_recv(j, ch, side):
         vs = pl.ds(ch * vc, vc)
         remote(
-            ys.at[j, side, vs], yh.at[j, side, vs], y_s.at[j, side, ch], y_r.at[j, side, ch],
+            ys.at[j, side, vs], yh.at[j, side, vs], y_s.at[j, side], y_r.at[j, side, ch],
             (partner, gy),
         ).wait_recv()
 
@@ -164,21 +181,27 @@
             return before if j else before & (h == 0)
         return after if j else after & (h == 1)
 
-    early = ret1.shape[2]
-    late = half - early
-
-    def back_copy(j, ch):
+    early = [half * EARLY[layer % len(EARLY)] // 32 * 8 for layer in range(lay)]
+    late = [half - e for e in early]
+
+    def back_copy(j, ch, layer):
         vs = pl.ds(ch * vc, vc)
-        dst = (ret1, ret2)[j - 1]
         return remote(
-            basis[j].at[vs, pl.ds(1 + theirs_at, lay), pl.ds(0, early)],
-            dst.at[vs], b_s.at[j - 1, ch], b_r.at[j - 1, ch], (partner, gy),
-        )
-
-    def late_copy(layer):
+            basis[j].at[vs, 1 + theirs_at + layer, pl.ds(0, early[layer])],
+            ret.at[j - 1, layer, vs, pl.ds(0, early[layer])],
+            b_s.at[layer], b_r.at[layer], (partner, gy),
+        )
+
+    def all_back(layer):
+        every = ret.at[:, layer, :, pl.ds(0, early[layer])]
+        return remote(every, every, b_s.at[layer], b_r.at[layer], (partner, gy))
+
+    def late_copy(layer, at):
         return remote(
-            held.at[:, pl.ds(layer, 1)],
-            out_ref.at[:, pl.ds(layer, 1), pl.ds(pl.multiple_of(hs + early, 8), late)],
+            held.at[:, pl.ds(layer, 1), pl.ds(0, late[layer])],
+            out_ref.at[
+                :, pl.ds(layer, 1), pl.ds(pl.multiple_of(at + early[layer], 8), late[layer])
+            ],
             l_s.at[layer], l_r.at[layer], (partner, gy),
         )
 
@@ -187,6 +210,8 @@
     )
 
     for ch in range(CHUNKS):
+        if ch:
+            load_r(ch).wait()
         exchange(0, ch).start()
 
         @pl.when((p == 0) & below)
@@ -197,7 +222,12 @@
         def _():
             z_from_rhs(ch, 1).start()
 
+    for v in range(blk):
+        rows_out[v] = jnp.where(
+            h == 0, r_ref[v, :, half - 1:half], r_ref[v, :, half:half + 1]
+        )
     load_d.wait()
+    rows_copy.start()
     diag_copy.start()
     for ch in range(CHUNKS):
         exchange(1, ch).start()
@@ -219,12 +249,16 @@
             return carry
         return run
 
+    known = (2 * ITERS - 1) * blk * blk
+    split = acc.shape[0] - 2 * blk * blk
+
     def keep_sum(moment, a, b, s):
         line = jnp.sum(s, axis=0, keepdims=True)
-        at = (moment * blk + a) * blk + b
+        first = moment * blk * blk + (split - known if moment >= 2 * ITERS - 1 else 0)
+        at = first + a * blk + b
         acc[at:at + 1] = line
         if a != b:
-            at = (moment * blk + b) * blk + a
+            at = first + b * blk + a
             acc[at:at + 1] = line
 
     zero = jnp.zeros((8, 128), jnp.float32)
@@ -263,14 +297,14 @@
             keep_sum(2 * j + 1, a, b, sums[i])
             keep_sum(2 * j + 2, a, b, sums[len(pairs) + i])
 
-    acc[7 * blk * blk:] = jnp.zeros((acc.shape[0] - 7 * blk * blk, 128), jnp.float32)
+    acc[known:split] = jnp.zeros((split - known, 128), jnp.float32)
     SC("gram0", gram_rhs)
 
     def relay(ch):
         remote(
             r_ref.at[pl.ds(0, vc), pl.ds(0, 1), pl.ds(os, half)],
             k0.at[pl.ds(ch * vc, vc), pl.ds(1 + (group_lay - 1) * (1 - p), 1)],
-            x_s.at[0, ch], x_r.at[0, ch], (partner, gy),
+            x_s, x_r.at[0, ch], (partner, gy),
         ).wait_recv()
 
         @pl.when((p == 0) & above)
@@ -295,7 +329,7 @@
         remote(
             r_ref.at[pl.ds(0, vc), pl.ds(0, 1), pl.ds(os, half)],
             k0.at[pl.ds(ch * vc, vc), pl.ds(1 + lay - p, 1)],
-            x_s.at[1, ch], x_r.at[1, ch], (partner, gy),
+            x_s, x_r.at[1, ch], (partner, gy),
         ).wait_recv()
 
         def run(v, carry):
@@ -307,6 +341,7 @@
         start_rows(0, ch)
 
     for ch in range(CHUNKS):
+        SC(f"wave#{ch}", lambda: wave(ch))
         SC(f"relay#{ch}", lambda: relay(ch))
 
     def rows_arrived():
@@ -340,14 +375,14 @@
             def _():
                 remote(
                     src.at[vs, pl.ds(1, 1)], src.at[vs, pl.ds(0, 1)],
-                    z_s.at[j, 1, ch], z_r.at[j, 1, ch], (partner, gy),
+                    z_s.at[j, 1], z_r.at[j, 1, ch], (partner, gy),
                 ).wait_recv()
 
             @pl.when(above)
             def _():
                 remote(
                     src.at[vs, pl.ds(1, 1)], src.at[vs, pl.ds(group_lay + 1, 1)],
-                    z_s.at[j, 0, ch], z_r.at[j, 0, ch], (partner, gy),
+                    z_s.at[j, 0], z_r.at[j, 0, ch], (partner, gy),
                 ).wait_recv()
 
         def row_waits():
@@ -395,30 +430,40 @@
             back_copy(*item).start()
         SC(f"gram{j}#{ch}", lambda: gram(j, ch))
 
+    def gather(first, last, skip):
+        count = last - first
+        sums = nt_dot(jnp.ones((8, 128), jnp.float32), acc[first:last])
+        lane_q = lax.broadcasted_iota(jnp.int32, (8, count), 1)
+        row_q = lax.broadcasted_iota(jnp.int32, (8, count), 0)
+        q = lax.broadcasted_iota(jnp.int32, (count, 128), 0) + (first - skip)
+        c = lax.broadcasted_iota(jnp.int32, (count, 128), 1)
+        pick = (q // (blk * blk) == c // blk) & (q % blk == c % blk)
+        kept = jnp.where((lane_q // blk) % blk == row_q, sums, 0.0)
+        return dot(kept, jnp.where(pick, 1.0, 0.0))
+
     for ch in range(CHUNKS):
         SC(f"arrived#{ch}", lambda: arrived(ch))
         apply(0, ch)
-    for j in range(1, ITERS):
-        for ch in range(CHUNKS):
-            apply(j, ch)
+    for ch in range(CHUNKS):
+        apply(1, ch)
+
+    def early_sums():
+        local = gather(0, split, 0)
+        mine[...] = local[:4] + pltpu.roll(local, 64, 1)[4:]
+
+    SC("early_sums", early_sums)
+    for ch in range(CHUNKS):
+        apply(2, ch)
 
     def reduce():
-        count = acc.shape[0]
-        sums = nt_dot(jnp.ones((8, 128), jnp.float32), acc[...])
-        lane_q = lax.broadcasted_iota(jnp.int32, (8, count), 1)
-        row_q = lax.broadcasted_iota(jnp.int32, (8, count), 0)
-        q = lax.broadcasted_iota(jnp.int32, (count, 128), 0)
-        c = lax.broadcasted_iota(jnp.int32, (count, 128), 1)
-        pick = (q // (blk * blk) == c // blk) & (q % blk == c % blk)
-        kept = jnp.where((lane_q // blk) % blk == row_q, sums, 0.0)
-        local = dot(kept, jnp.where(pick, 1.0, 0.0))
-        packed = local[:4] + pltpu.roll(local, 64, 1)[4:]
+        local = gather(split, acc.shape[0], split - known)
+        packed = mine[...] + local[:4] + pltpu.roll(local, 64, 1)[4:]
         mine[...] = packed
         slots[me] = packed
 
         def send(off, carry):
             to = (me + off) % n_dev
-            remote(mine, slots.at[me], g_s.at[to], g_r.at[me], device(to)).start()
+            remote(mine, slots.at[me], g_s, g_r, device(to)).start()
             return carry
 
         lax.fori_loop(1, n_dev, send, 0)
@@ -428,12 +473,8 @@
     SC("red_send", reduce)
 
     def collect():
-        def take(off, carry):
-            frm = (me + off) % n_dev
-            remote(mine, slots.at[frm], g_s.at[frm], g_r.at[frm], device(frm)).wait()
-            return carry
-
-        lax.fori_loop(1, n_dev, take, 0)
+        others = slots.at[pl.ds(0, n_dev - 1)]
+        remote(others, others, g_s, g_r, (partner, gy)).wait()
 
     SC("red_wait", collect)
     packed = jnp.sum(slots[...], axis=0)
@@ -444,22 +485,16 @@
     moments = keep(
         jnp.concatenate([packed, pltpu.roll(packed, 64, 1)], axis=0), 0, 64
     )
+    small, order = ITERS * blk, (ITERS + 1) * blk
+    inv = 1.0 / SCALE
+
     def solve():
-        order = (ITERS + 1) * blk
-        lane32 = lax.broadcasted_iota(jnp.int32, (order, 128), 1)
-        row32 = lax.broadcasted_iota(jnp.int32, (order, 128), 0)
-        full = jnp.concatenate(
-            [keep(left_by(moments, blk * i), 0, order) for i in range(ITERS + 1)], axis=0
-        )
-        full = full + jnp.where(lane32 == row32 + order, 1.0, 0.0)
-        inv = 1.0 / SCALE
         second = (
             (inv * inv) * left_by(moments, 2 * blk)
             + (2.0 * CENTRE * inv) * left_by(moments, blk)
             + (CENTRE * CENTRE) * moments
         )
         target = inv * left_by(moments, blk) + CENTRE * moments
-        small = ITERS * blk
         normal = jnp.concatenate(
             [
                 keep(left_by(second, blk * i), 0, small)
@@ -469,12 +504,23 @@
             axis=0,
         )
         rows_small = lax.broadcasted_iota(jnp.int32, (small, 1), 0)
+        for k in range(small):
+            row = normal[k:k + 1] / normal[k:k + 1, k:k + 1]
+            column = jnp.where(rows_small == k, 0.0, normal[:, k:k + 1])
+            normal = jnp.where(rows_small == k, row, normal - column * row)
+        return normal
+
+    normal = SC("solve", solve)
+
+    def factor():
+        lane32 = lax.broadcasted_iota(jnp.int32, (order, 128), 1)
+        row32 = lax.broadcasted_iota(jnp.int32, (order, 128), 0)
+        full = jnp.concatenate(
+            [keep(left_by(moments, blk * i), 0, order) for i in range(ITERS + 1)], axis=0
+        )
+        full = full + jnp.where(lane32 == row32 + order, 1.0, 0.0)
         rows_full = lax.broadcasted_iota(jnp.int32, (order, 1), 0)
         for k in range(order):
-            if k < small:
-                row = normal[k:k + 1] / normal[k:k + 1, k:k + 1]
-                column = jnp.where(rows_small == k, 0.0, normal[:, k:k + 1])
-                normal = jnp.where(rows_small == k, row, normal - column * row)
             row = full[k:k + 1] / full[k:k + 1, k:k + 1]
             column = jnp.where(rows_full <= k, 0.0, full[:, k:k + 1])
             full = full - column * row
@@ -484,17 +530,10 @@
         lower_inv = left_by(full, order)
         lower_inv = jnp.where(lane32 < small, lower_inv, 0.0)[:small]
         hess = inv * nt_dot(pltpu.roll(lower_inv, blk, 1), upper)
-        eye = lax.broadcasted_iota(jnp.int32, (small, order), 0) == lax.broadcasted_iota(
-            jnp.int32, (small, order), 1
-        )
-        row_b = lax.broadcasted_iota(jnp.int32, (small, order), 0) // blk
-        col_b = lax.broadcasted_iota(jnp.int32, (small, order), 1) // blk
-        hess = hess + jnp.where(eye, CENTRE, 0.0)
-        hess_ref[...] = jnp.where(col_b <= row_b + 1, hess, 0.0)
-        return normal
-
-    normal = SC("solve", solve)
-    small = ITERS * blk
+        row_h = lax.broadcasted_iota(jnp.int32, (small, order), 0)
+        col_h = lax.broadcasted_iota(jnp.int32, (small, order), 1)
+        hess = hess + jnp.where(row_h == col_h, CENTRE, 0.0)
+        hess_ref[...] = jnp.where(col_h // blk <= row_h // blk + 1, hess, 0.0)
 
     def spread():
         for k in range(small):
@@ -516,7 +555,11 @@
                 vals = []
                 for ref, l_at, base in sources:
                     first_row = pl.multiple_of(base + t * 8, 8)
-                    vals += [ref[v, l_at + layer, pl.ds(first_row, 8), cols] for v in range(blk)]
+                    vals += [
+                        ref[v, pl.ds(first_row, 8), cols] if l_at is None
+                        else ref[v, l_at + layer, pl.ds(first_row, 8), cols]
+                        for v in range(blk)
+                    ]
                 for u in range(blk):
                     total = splat[u] * vals[0]
                     for k in range(1, small):
@@ -528,8 +571,11 @@
 
     def send_late():
         for layer in range(lay):
-            combine(held, (layer, layer + 1), 0, late, [(k, 1 + theirs_at, early) for k in basis[:ITERS]])
-            late_copy(layer).start()
+            combine(
+                held, (layer, layer + 1), 0, late[layer],
+                [(k, 1 + theirs_at, early[layer]) for k in basis[:ITERS]],
+            )
+            late_copy(layer, hs).start()
 
     SC("comb_late", send_late)
     SC("comb_own", lambda: combine(
@@ -537,66 +583,74 @@
     ))
 
     def back_wait():
-        for j in (1, 2):
-            for ch in range(CHUNKS):
-                back_copy(j, ch).wait()
+        for layer in range(lay):
+            all_back(layer).wait()
 
     SC("back_wait", back_wait)
-    SC("comb_other", lambda: combine(
-        out_ref, (0, lay), os, early, ((r_ref, 0, os), (ret1, 0, 0), (ret2, 0, 0))
-    ))
-
-    def late_wait():
+
+    def rest():
         for layer in range(lay):
-            late_copy(layer).wait_send()
-            remote(
-                held.at[:, pl.ds(layer, 1)],
-                out_ref.at[:, pl.ds(layer, 1), pl.ds(pl.multiple_of(os + early, 8), late)],
-                l_s.at[layer], l_r.at[layer], (partner, gy),
-            ).wait_recv()
-
-    SC("late_wait", late_wait)
-
-    for ch in range(CHUNKS):
-        for which in (0, 1):
-            exchange(which, ch).wait_send()
-
-        @pl.when(below)
-        def _():
-            z_copy(0, ch, 0).wait_send()
-
-        @pl.when(above)
-        def _():
-            z_copy(0, ch, 1).wait_send()
-
-        for j in range(1, ITERS):
-            @pl.when(below)
-            def _():
-                z_copy(j, ch, 0).wait_send()
-
-            @pl.when(above)
-            def _():
-                z_copy(j, ch, 1).wait_send()
-
+            combine(
+                out_ref, (layer, layer + 1), os, early[layer],
+                ((r_ref, 0, os), (ret.at[0, layer], None, 0), (ret.at[1, layer], None, 0)),
+            )
+
+    SC("comb_other", rest)
+    SC("factor", factor)
+
+    def drain():
+        whole = r_ref.at[:, :, pl.ds(os, half)]
+        remote(whole, whole, x_s, x_r.at[0, 0], (partner, gy)).wait_send()
         for j in range(ITERS):
+            for direction, there in ((0, below), (1, above)):
+                @pl.when(there)
+                def _():
+                    every = basis[j].at[:, pl.ds(0, 1)]
+                    remote(
+                        every, every, z_s.at[j, direction], z_r.at[j, direction, 0], (partner, gy)
+                    ).wait_send()
+
             for side in range(2):
                 @pl.when(has(j, side))
                 def _():
-                    y_copy(j, ch, side).wait_send()
-
-    diag_copy.wait_send()
+                    every = ys.at[j, side]
+                    remote(
+                        every, every, y_s.at[j, side], y_r.at[j, side, 0], (partner, gy)
+                    ).wait_send()
+
+        diag_copy.wait_send()
+
+    SC("drain", drain)
+
+    def late_wait():
+        for layer in range(lay):
+            late_copy(layer, hs).wait_send()
+            late_copy(layer, os).wait_recv()
+
+    SC("late_wait", late_wait)
+
+
+def store(x_ref, h_ref, x_out, h_out, sems):
+    copies = (
+        pltpu.make_async_copy(x_ref, x_out, sems.at[0]),
+        pltpu.make_async_copy(h_ref, h_out, sems.at[1]),
+    )
+    for copy in copies:
+        copy.start()
+    for copy in copies:
+        copy.wait()
 
 
 def body(right_side, diagonal):
     blk, lay, rows, nx = right_side.shape
     half, group_lay = rows // 2, 2 * lay
-    early = half * EARLY // 32 * 8
+    early = [half * EARLY[layer % len(EARLY)] // 32 * 8 for layer in range(lay)]
     n_z, n_y = lax.axis_size("gz"), lax.axis_size("gy")
     vmem = lambda *shape: pltpu.VMEM(shape, jnp.float32)
-    dma = lambda *shape: pltpu.SemaphoreType.DMA(shape)
+    dma = lambda *shape: pltpu.SemaphoreType.DMA(shape) if shape else pltpu.SemaphoreType.DMA
     small, order = ITERS * blk, (ITERS + 1) * blk
     in_hbm = lambda x: pltpu.with_memory_space_constraint(x, pltpu.HBM)
-    return pl.pallas_call(
+    x, h = pl.pallas_call(
         kernel,
         out_shape=(vmem(*right_side.shape), vmem(small, order)),
         in_specs=[pl.BlockSpec(memory_space=pltpu.HBM)] * 2,
@@ -609,9 +663,8 @@
             vmem(blk, group_lay + 2, half, nx),
             vmem(blk, group_lay, half, nx),
             vmem(group_lay, half, nx),
-            vmem(blk, lay, early, nx),
-            vmem(blk, lay, early, nx),
-            vmem(blk, lay, half - early, nx),
+            vmem(ITERS - 1, lay, blk, max(early), nx),
+            vmem(blk, lay, half - min(early), nx),
             vmem(ITERS, 2, blk, group_lay, nx),
             vmem(ITERS, 2, blk, group_lay, nx),
             vmem(blk, lay, 1, nx),
@@ -620,20 +673,32 @@
             vmem(4, 128),
             vmem(n_z * n_y, 4, 128),
             vmem(small * blk, 8, 128),
-            dma(2),
-            dma(2, CHUNKS), dma(2, CHUNKS),
-            pltpu.SemaphoreType.DMA, pltpu.SemaphoreType.DMA,
-            dma(ITERS, 2, CHUNKS), dma(ITERS, 2, CHUNKS),
-            dma(ITERS, 2, CHUNKS), dma(ITERS, 2, CHUNKS),
-            pltpu.SemaphoreType.DMA, pltpu.SemaphoreType.DMA,
-            dma(2, CHUNKS), dma(2, CHUNKS), dma(lay), dma(lay),
-            dma(n_z * n_y), dma(n_z * n_y),
+            dma(CHUNKS + 1), pltpu.SemaphoreType.REGULAR((4,)),
+            dma(), dma(2, CHUNKS),
+            dma(), dma(),
+            dma(ITERS, 2), dma(ITERS, 2, CHUNKS),
+            dma(ITERS, 2), dma(ITERS, 2, CHUNKS),
+            dma(), dma(),
+            dma(lay), dma(lay), dma(lay), dma(lay),
+            dma(), dma(),
         ],
         compiler_params=pltpu.CompilerParams(
             collective_id=0, has_side_effects=True, vmem_limit_bytes=40 * 1024 * 1024
         ),
         name="gmres",
     )(in_hbm(right_side), in_hbm(diagonal))
+    in_vmem = lambda x: pltpu.with_memory_space_constraint(x, pltpu.VMEM)
+    return pl.pallas_call(
+        store,
+        out_shape=(
+            jax.ShapeDtypeStruct(x.shape, jnp.float32), jax.ShapeDtypeStruct(h.shape, jnp.float32),
+        ),
+        in_specs=[pl.BlockSpec(memory_space=pltpu.VMEM)] * 2,
+        out_specs=(pl.BlockSpec(memory_space=pltpu.HBM),) * 2,
+        scratch_shapes=[dma(2)],
+        compiler_params=pltpu.CompilerParams(vmem_limit_bytes=4 * 1024 * 1024),
+        name="store",
+    )(in_vmem(x), in_vmem(h))
 
 
 def solution(mesh):

time: 83.1 us -> 74.5 us (0.90)
  Pallas kernels: 80.4 us -> 73.7 us
  local copies, waits for them, and re-layouts: 1.92 us -> 0 us
    pallas_call x1, Pallas kernels: 80.4 us -> 72.3 us  [body(): pl.pallas_call(kernel, out_shape=(vmem(*right_side.shape), vmem(small, or...]
    unnamed x2 -> x0, local copies, waits for them, and re-layouts: 1.92 us -> none
    pallas_call x0 -> x1, Pallas kernels: none -> 1.34 us  [body(): pl.pallas_call(store, out_shape=(jax.ShapeDtypeStruct(x.shape, jnp.float3...]
where the time goes in v2:
time: 74.5 us; the launch traced here: 74.3 us
  Pallas kernels  73.7 us (99%)
    pallas_call x1, Pallas kernels, body(): pl.pallas_call(kernel, out_shape=(vmem(*right_side.shape), vmem(small, or...  72.3 us

profile of v2, /device:TPU:0, one launch (start us, length us, event | category | flops | bytes accessed | tf_op | source)
XLA Modules:
  0.0 74.3 jit_solution(3166568180702795954)
XLA Ops:
  0.6 72.3 %gmres.1 = (f32[8,2,64,512]{3,2,1,0:T(8,128)S(1)}, f32[24,32]{1,0:T(8,128)S(1)}) custom-call(f32[8,2,64,512]{3,2,1,0:T(8,128)} %r_hbm.1, f32[2,64,512]{2,1,0:T(8,128)} %d_hbm.1), custom_call_target="tpu_custom_call" | custom-call | tf_op jit(solution)/shard_map/gmres/pallas_call | solution.py:653
  73.0 1.3 %store.1 = (f32[8,2,64,512]{3,2,1,0:T(8,128)}, f32[24,32]{1,0:T(8,128)}) custom-call(f32[8,2,64,512]{3,2,1,0:T(8,128)S(1)} %get-tuple-element.4.x_ref, f32[24,32]{1,0:T(8,128)S(1)} %get-tuple-element.5.h_ref), custom_call_target="tpu_custom_call" | custom-call | tf_op jit(solution)/shard_map/store/pallas_call | solution.py:691

commit v3 on v2

--- a/solution.py
+++ b/solution.py
@@ -10,14 +10,15 @@
 ITERS = 3
 CENTRE = 7.5
 SCALE = 0.25
-CHUNKS = 4
-EARLY = (3, 2)
+CUTS = (0, 1, 3, 5, 7, 8)
+CHUNKS = len(CUTS) - 1
+EARLY = (1, 1)
 BACK = {
-    (0, 1): ((1, 0, 0),), (0, 2): ((1, 0, 1), (1, 1, 0)), (0, 3): ((1, 1, 1), (1, 2, 0)),
-    (1, 0): ((1, 2, 1),), (1, 2): ((1, 3, 0),), (1, 3): ((1, 3, 1),),
-    (2, 0): ((2, 0, 0), (2, 0, 1)), (2, 1): ((2, 1, 0),),
-    "reduce": ((2, 1, 1), (2, 2, 0), (2, 2, 1), (2, 3, 0), (2, 3, 1)),
+    (0, 1): ("ghost",), (0, 2): ((0, 0),), (0, 3): ((0, 1),), (0, 4): ((0, 2),), (1, 1): ((0, 3),),
+    (1, 4): ((0, 4), (1, 0)), (2, 0): ((1, 1),), (2, 1): ((1, 2),),
+    "reduce": ((1, 3), (1, 4), (2, 0), (2, 1), (2, 2), (2, 3), (2, 4)),
 }
+RELAY = {(2, 1): (0,), "reduce": (1, 2, 3, 4)}
 MESH = pl.DeviceIdType.MESH
 HIGH = lax.Precision.HIGHEST
 
@@ -40,12 +41,15 @@
 def kernel(
     r_hbm, d_hbm, out_ref, hess_ref,
     r_ref, d_ref, k0, k1, k2, k3, diag, ret, held, ys, yh, rows_out, rows_in,
+    deep, d_deep, g_out, g_in, kd1, kd2,
     acc, mine, slots, splat, i_s, met,
     x_s, x_r, d_s, d_r, z_s, z_r, y_s, y_r, e_s, e_r, b_s, b_r, l_s, l_r, g_s, g_r,
+    q_s, q_r, qz_s, qz_r, w_s, w_r,
 ):
     blk, lay, rows, nx = r_ref.shape
     half, group_lay = rows // 2, 2 * lay
-    vc = blk // CHUNKS
+    starts = [blk * cut // CUTS[-1] for cut in CUTS]
+    part = lambda ch: pl.ds(starts[ch], starts[ch + 1] - starts[ch])
     n_z, n_y = lax.axis_size("gz"), lax.axis_size("gy")
     gz, gy = lax.axis_index("gz"), lax.axis_index("gy")
     n_dev = n_z * n_y
@@ -64,6 +68,17 @@
     next_dev = (gz + (1 - h) * (partner - gz), gy + h)
     basis = (k0, k1, k2, k3)
     edge = (lay - 1) * p
+    inner = half // 2
+    outer = half - inner
+    early = [outer * EARLY[layer % len(EARLY)] // 16 * 8 for layer in range(lay)]
+    late = [outer - e for e in early]
+    theirs_out = pl.multiple_of(h * inner, 8)
+    mine_out = pl.multiple_of((1 - h) * inner, 8)
+    inner_at = pl.multiple_of(os + h * outer, 8)
+    far, near_l = (lay - 1) * p, (lay - 1) * (1 - p)
+    beyond = jnp.where(p == 0, below, above)
+    onward = jnp.where(p == 0, above, below)
+    onward_dev = (gz + 2 - 4 * p, gy)
 
     def remote(src, dst, send, recv, dev):
         return pltpu.make_async_remote_copy(
@@ -75,7 +90,7 @@
         return (i // n_y, i % n_y)
 
     def load_r(ch):
-        vs = pl.ds(ch * vc, vc)
+        vs = part(ch)
         return pltpu.make_async_copy(r_hbm.at[vs], r_ref.at[vs], i_s.at[ch])
 
     load_d = pltpu.make_async_copy(d_hbm, d_ref, i_s.at[CHUNKS])
@@ -126,6 +141,12 @@
     def _():
         yh[:, 1] = jnp.zeros((ITERS,) + yh.shape[2:], jnp.float32)
 
+    @pl.when(jnp.logical_not(beyond))
+    def _():
+        deep[0:2] = jnp.zeros((2,) + deep.shape[1:], jnp.float32)
+        d_deep[0] = jnp.zeros(d_deep.shape[1:], jnp.float32)
+        g_in[:, 0] = jnp.zeros((blk, 1, nx), jnp.float32)
+
     load_r(0).wait()
     SC("barrier", lambda: pl.semaphore_wait(
         barrier, 1 + sum(jnp.where(there, 1, 0) for there, _ in sides)
@@ -134,7 +155,7 @@
 
     def exchange(which, ch):
         layer = edge + which * (1 - 2 * p)
-        vs = pl.ds(ch * vc, vc)
+        vs = part(ch)
         return remote(
             r_ref.at[vs, pl.ds(layer, 1), pl.ds(os, half)],
             k0.at[vs, pl.ds(1 + mine_at + layer, 1)],
@@ -142,37 +163,37 @@
         )
 
     def z_from_rhs(ch, direction):
-        vs = pl.ds(ch * vc, vc)
+        vs = part(ch)
         if direction == 0:
             dst, dev = k0.at[vs, pl.ds(group_lay + 1, 1)], (gz - 2, gy)
         else:
             dst, dev = k0.at[vs, pl.ds(0, 1)], (gz + 2, gy)
         return remote(
             r_ref.at[vs, pl.ds(edge, 1), pl.ds(hs, half)], dst,
-            z_s.at[0, direction], z_r.at[0, direction, ch], dev,
+            z_s.at[direction], z_r.at[0, direction, ch], dev,
         )
 
     def z_copy(j, ch, direction):
-        vs = pl.ds(ch * vc, vc)
+        vs = part(ch)
         k = basis[j]
         if direction == 0:
             src, dst, dev = k.at[vs, pl.ds(1, 1)], k.at[vs, pl.ds(group_lay + 1, 1)], (gz - 2, gy)
         else:
             src, dst, dev = k.at[vs, pl.ds(group_lay, 1)], k.at[vs, pl.ds(0, 1)], (gz + 2, gy)
-        return remote(src, dst, z_s.at[j, direction], z_r.at[j, direction, ch], dev)
+        return remote(src, dst, z_s.at[direction], z_r.at[j % 2, direction, ch], dev)
 
     def y_copy(j, ch, side):
-        vs = pl.ds(ch * vc, vc)
+        vs = part(ch)
         dev = prev_dev if side == 0 else next_dev
         return remote(
             ys.at[j, side, vs], yh.at[j, 1 - side, vs],
-            y_s.at[j, side], y_r.at[j, 1 - side, ch], dev,
+            y_s.at[side], y_r.at[j % 2, 1 - side, ch], dev,
         )
 
     def y_wait_recv(j, ch, side):
-        vs = pl.ds(ch * vc, vc)
+        vs = part(ch)
         remote(
-            ys.at[j, side, vs], yh.at[j, side, vs], y_s.at[j, side], y_r.at[j, side, ch],
+            ys.at[j, side, vs], yh.at[j, side, vs], y_s.at[side], y_r.at[j % 2, side, ch],
             (partner, gy),
         ).wait_recv()
 
@@ -181,29 +202,89 @@
             return before if j else before & (h == 0)
         return after if j else after & (h == 1)
 
-    early = [half * EARLY[layer % len(EARLY)] // 32 * 8 for layer in range(lay)]
-    late = [half - e for e in early]
-
-    def back_copy(j, ch, layer):
-        vs = pl.ds(ch * vc, vc)
-        return remote(
-            basis[j].at[vs, 1 + theirs_at + layer, pl.ds(0, early[layer])],
-            ret.at[j - 1, layer, vs, pl.ds(0, early[layer])],
-            b_s.at[layer], b_r.at[layer], (partner, gy),
-        )
+    def back_copy(j, ch):
+        vs = part(ch)
+        return [
+            remote(
+                basis[j].at[vs, 1 + theirs_at + layer, pl.ds(theirs_out, early[layer])],
+                ret.at[j - 1, layer, vs, pl.ds(0, early[layer])],
+                b_s.at[layer], b_r.at[layer], (partner, gy),
+            )
+            for layer in range(lay)
+        ]
 
     def all_back(layer):
         every = ret.at[:, layer, :, pl.ds(0, early[layer])]
         return remote(every, every, b_s.at[layer], b_r.at[layer], (partner, gy))
 
-    def late_copy(layer, at):
+    def late_copy(layer, at, first, count):
         return remote(
-            held.at[:, pl.ds(layer, 1), pl.ds(0, late[layer])],
+            held.at[:, pl.ds(layer, 1), pl.ds(first, count)],
             out_ref.at[
-                :, pl.ds(layer, 1), pl.ds(pl.multiple_of(at + early[layer], 8), late[layer])
+                :, pl.ds(layer, 1), pl.ds(pl.multiple_of(at + early[layer] + first, 8), count)
             ],
             l_s.at[layer], l_r.at[layer], (partner, gy),
         )
+
+    give_at = pl.multiple_of(hs + (1 - h) * outer, 8)
+
+    def deep_copy(ch):
+        vs = part(ch)
+        return [
+            remote(
+                r_ref.at[vs, layer, pl.ds(give_at, inner)], deep.at[slot, vs],
+                q_s, q_r.at[ch], (partner, gy),
+            )
+            for slot, layer in ((2, near_l), (3, far))
+        ]
+
+    def deep_recv(ch):
+        every = deep.at[pl.ds(2, 2), part(ch)]
+        return remote(every, every, q_s, q_r.at[ch], (partner, gy))
+
+    def deep_relay(ch):
+        vs = part(ch)
+        return remote(
+            deep.at[pl.ds(2, 2), vs], deep.at[pl.ds(0, 2), vs], qz_s, qz_r.at[ch], onward_dev
+        )
+
+    ghost_copies = [
+        remote(g_out, g_in.at[:, pl.ds(1, 2)], w_s.at[0], w_r.at[0], (partner, gy))
+    ] + [
+        remote(
+            d_ref.at[layer, pl.ds(give_at, inner)], d_deep.at[slot], w_s.at[1], w_r.at[1],
+            (partner, gy),
+        )
+        for slot, layer in ((1, near_l), (2, far))
+    ]
+    both_diag = d_deep.at[pl.ds(1, 2)]
+    ghost_diag = remote(both_diag, both_diag, w_s.at[1], w_r.at[1], (partner, gy))
+    ghost_relays = (
+        remote(g_in.at[:, pl.ds(2, 1)], g_in.at[:, pl.ds(0, 1)], w_s.at[2], w_r.at[2], onward_dev),
+        remote(d_deep.at[pl.ds(2, 1)], d_deep.at[pl.ds(0, 1)], w_s.at[3], w_r.at[3], onward_dev),
+    )
+
+    def issue(items):
+        for item in items:
+            if item == "ghost":
+                copies = ghost_copies
+            else:
+                copies = back_copy(*item) if item[0] else deep_copy(item[1])
+            for copy in copies:
+                copy.start()
+
+    def relay_deep(ch):
+        deep_recv(ch).wait_recv()
+        if ch == 0:
+            ghost_copies[0].wait_recv()
+            ghost_diag.wait_recv()
+
+        @pl.when(onward)
+        def _():
+            deep_relay(ch).start()
+            if ch == 0:
+                for copy in ghost_relays:
+                    copy.start()
 
     diag_copy = remote(
         d_ref.at[:, pl.ds(os, half)], diag.at[pl.ds(mine_at, lay)], d_s, d_r, (partner, gy)
@@ -226,6 +307,10 @@
         rows_out[v] = jnp.where(
             h == 0, r_ref[v, :, half - 1:half], r_ref[v, :, half:half + 1]
         )
+        for slot, layer in ((0, near_l), (1, far)):
+            g_out[v, slot] = jnp.where(
+                h == 0, r_ref[v, layer, outer - 1:outer], r_ref[v, layer, half + inner:half + inner + 1]
+            )
     load_d.wait()
     rows_copy.start()
     diag_copy.start()
@@ -279,8 +364,8 @@
     def gram(j, ch):
         src, dst = basis[j], basis[j + 1]
         shift = 0 if j == ITERS - 1 else 1
-        top = (ch + 1) * vc
-        pairs = [(a, b) for b in range(ch * vc, top) for a in range(b + 1)]
+        top = starts[ch + 1]
+        pairs = [(a, b) for b in range(starts[ch], top) for a in range(b + 1)]
 
         def body(sums, layer, at, cols):
             x = [src[v, 1 + layer, pl.ds(at, 8), cols] for v in range(top)]
@@ -302,8 +387,8 @@
 
     def relay(ch):
         remote(
-            r_ref.at[pl.ds(0, vc), pl.ds(0, 1), pl.ds(os, half)],
-            k0.at[pl.ds(ch * vc, vc), pl.ds(1 + (group_lay - 1) * (1 - p), 1)],
+            r_ref.at[part(ch), pl.ds(0, 1), pl.ds(os, half)],
+            k0.at[part(ch), pl.ds(1 + (group_lay - 1) * (1 - p), 1)],
             x_s, x_r.at[0, ch], (partner, gy),
         ).wait_recv()
 
@@ -327,8 +412,8 @@
 
     def arrived(ch):
         remote(
-            r_ref.at[pl.ds(0, vc), pl.ds(0, 1), pl.ds(os, half)],
-            k0.at[pl.ds(ch * vc, vc), pl.ds(1 + lay - p, 1)],
+            r_ref.at[part(ch), pl.ds(0, 1), pl.ds(os, half)],
+            k0.at[part(ch), pl.ds(1 + lay - p, 1)],
             x_s, x_r.at[1, ch], (partner, gy),
         ).wait_recv()
 
@@ -337,11 +422,12 @@
                 stage_rows(0, v, layer, k0[v, 1 + layer])
             return carry
 
-        lax.fori_loop(ch * vc, (ch + 1) * vc, run, 0)
+        lax.fori_loop(starts[ch], starts[ch + 1], run, 0)
         start_rows(0, ch)
 
     for ch in range(CHUNKS):
-        SC(f"wave#{ch}", lambda: wave(ch))
+        if ch < len(sides):
+            SC(f"wave#{ch}", lambda: wave(ch))
         SC(f"relay#{ch}", lambda: relay(ch))
 
     def rows_arrived():
@@ -368,21 +454,21 @@
     def apply(j, ch):
         src, dst = basis[j], basis[j + 1]
         shift = 0 if j == ITERS - 1 else 1
-        vs = pl.ds(ch * vc, vc)
+        vs = part(ch)
 
         def waits():
             @pl.when(below)
             def _():
                 remote(
                     src.at[vs, pl.ds(1, 1)], src.at[vs, pl.ds(0, 1)],
-                    z_s.at[j, 1], z_r.at[j, 1, ch], (partner, gy),
+                    z_s.at[1], z_r.at[j % 2, 1, ch], (partner, gy),
                 ).wait_recv()
 
             @pl.when(above)
             def _():
                 remote(
                     src.at[vs, pl.ds(1, 1)], src.at[vs, pl.ds(group_lay + 1, 1)],
-                    z_s.at[j, 0], z_r.at[j, 0, ch], (partner, gy),
+                    z_s.at[0], z_r.at[j % 2, 0, ch], (partner, gy),
                 ).wait_recv()
 
         def row_waits():
@@ -391,6 +477,8 @@
                 def _():
                     y_wait_recv(j, ch, side)
 
+        for which in RELAY.get((j, ch), ()):
+            SC(f"drelay#{which}", lambda: relay_deep(which))
         SC(f"z_wait{j}#{ch}", waits)
         SC(f"y_wait{j}#{ch}", row_waits)
 
@@ -415,7 +503,7 @@
                     stage_rows(j + 1, v, layer, value)
             return carry
 
-        SC(f"apply{j}#{ch}", lambda: lax.fori_loop(ch * vc, (ch + 1) * vc, run, 0))
+        SC(f"apply{j}#{ch}", lambda: lax.fori_loop(starts[ch], starts[ch + 1], run, 0))
         if j < ITERS - 1:
             @pl.when(below)
             def _():
@@ -426,8 +514,7 @@
                 z_copy(j + 1, ch, 1).start()
 
             start_rows(j + 1, ch)
-        for item in BACK.get((j, ch), ()):
-            back_copy(*item).start()
+        issue(BACK.get((j, ch), ()))
         SC(f"gram{j}#{ch}", lambda: gram(j, ch))
 
     def gather(first, last, skip):
@@ -441,6 +528,85 @@
         kept = jnp.where((lane_q // blk) % blk == row_q, sums, 0.0)
         return dot(kept, jnp.where(pick, 1.0, 0.0))
 
+    row_d = lax.broadcasted_iota(jnp.int32, (inner, nx), 0)
+    col_d = lax.broadcasted_iota(jnp.int32, (inner, nx), 1)
+
+    def sideways(here, col):
+        return jnp.where(col == 0, 0.0, pltpu.roll(here, 1, 1)) + jnp.where(
+            col == nx - 1, 0.0, pltpu.roll(here, nx - 1, 1)
+        )
+
+    def deepen(ch):
+        @pl.when(beyond)
+        def _():
+            every = deep.at[pl.ds(0, 2), part(ch)]
+            remote(every, every, qz_s, qz_r.at[ch], (partner, gy)).wait_recv()
+            if ch == 0:
+                for slot, ref in ((2, g_in.at[:, pl.ds(0, 1)]), (3, d_deep.at[pl.ds(0, 1)])):
+                    remote(ref, ref, w_s.at[slot], w_r.at[slot], (partner, gy)).wait_recv()
+
+        edge_of = lambda ref, v, slot: jnp.where(
+            h == 0, ref[v, slot, half - 1:half], ref[v, slot, 0:1]
+        )
+        ghost_of = lambda row: jnp.where(
+            h == 0, row(half + inner), row(outer - 1)
+        )
+        after_of = lambda row: jnp.where(
+            h == 0, row(half + inner + 1), row(outer - 2)
+        )
+        slots = {
+            "beyond": (group_lay + 1) * p, "far": 1 + (group_lay - 1) * p,
+            "near": lay + p, "next": lay + 1 - p,
+        }
+        d_far, d_near = d_ref[far, pl.ds(inner_at, inner)], d_ref[near_l, pl.ds(inner_at, inner)]
+        g_far = ghost_of(lambda i: d_ref[far, i:i + 1])
+        g_near = ghost_of(lambda i: d_ref[near_l, i:i + 1])
+        exists = jnp.where(beyond, 1.0, 0.0)
+        one_col = lax.broadcasted_iota(jnp.int32, (1, nx), 1)
+
+        def block(here, below_z, above_z, edge_row, ghost_row, extra):
+            up = jnp.where(
+                row_d == 0, jnp.where(h == 0, edge_row, ghost_row), pltpu.roll(here, 1, 0)
+            )
+            down = jnp.where(
+                row_d == inner - 1, jnp.where(h == 0, ghost_row, edge_row),
+                pltpu.roll(here, inner - 1, 0),
+            )
+            near = (below_z + above_z) + (up + down) + sideways(here, col_d)
+            return SCALE * (((6.0 - CENTRE) + extra) * here - near)
+
+        def run(v, carry):
+            r_far = r_ref[v, far, pl.ds(inner_at, inner)]
+            r_near = r_ref[v, near_l, pl.ds(inner_at, inner)]
+            two, one, nxt, last = deep[0, v], deep[1, v], deep[2, v], deep[3, v]
+            ghost_far = ghost_of(lambda i: r_ref[v, far, i:i + 1])
+            ghost_near = ghost_of(lambda i: r_ref[v, near_l, i:i + 1])
+            ghost_one, ghost_next = g_in[v, 0], g_in[v, 1]
+            rows_of = lambda which: edge_of(k0, v, slots[which])
+            k_one = exists * block(one, two, r_far, rows_of("beyond"), ghost_one, d_deep[0])
+            k_far = block(r_far, one, r_near, rows_of("far"), ghost_far, d_far)
+            k_near = block(r_near, r_far, nxt, rows_of("near"), ghost_near, d_near)
+            k_next = block(nxt, r_near, last, rows_of("next"), ghost_next, d_deep[1])
+
+            def line(here, inside, layer, beside, extra):
+                outside = after_of(lambda i: r_ref[v, layer, i:i + 1])
+                within = jnp.where(h == 0, inside[inner - 1:inner], inside[0:1])
+                near = beside + (outside + within) + sideways(here, one_col)
+                return SCALE * (((6.0 - CENTRE) + extra) * here - near)
+
+            line_far = line(ghost_far, r_far, far, ghost_one + ghost_near, g_far)
+            line_near = line(ghost_near, r_near, near_l, ghost_far + ghost_next, g_near)
+            kd1[0, v], kd1[1, v] = k_far, k_near
+            kd2[0, v] = block(
+                k_far, k_one, k_near, edge_of(k1, v, slots["far"]), line_far, d_far
+            )
+            kd2[1, v] = block(
+                k_near, k_far, k_next, edge_of(k1, v, slots["near"]), line_near, d_near
+            )
+            return carry
+
+        lax.fori_loop(starts[ch], starts[ch + 1], run, 0)
+
     for ch in range(CHUNKS):
         SC(f"arrived#{ch}", lambda: arrived(ch))
         apply(0, ch)
@@ -456,7 +622,11 @@
         apply(2, ch)
 
     def reduce():
-        local = gather(split, acc.shape[0], split - known)
+        lane_s = lax.broadcasted_iota(jnp.int32, (8, 128), 1)
+        local = jnp.zeros((8, 128), jnp.float32)
+        for i in range(2 * blk):
+            column = jnp.sum(acc[split + i * blk:split + (i + 1) * blk], axis=1, keepdims=True)
+            local = local + jnp.where(lane_s == known // blk + i, column, 0.0)
         packed = mine[...] + local[:4] + pltpu.roll(local, 64, 1)[4:]
         mine[...] = packed
         slots[me] = packed
@@ -467,8 +637,9 @@
             return carry
 
         lax.fori_loop(1, n_dev, send, 0)
-        for item in BACK.get("reduce", ()):
-            back_copy(*item).start()
+        issue(BACK.get("reduce", ()))
+        for which in RELAY.get("reduce", ()):
+            relay_deep(which)
 
     SC("red_send", reduce)
 
@@ -476,6 +647,7 @@
         others = slots.at[pl.ds(0, n_dev - 1)]
         remote(others, others, g_s, g_r, (partner, gy)).wait()
 
+    SC("deepen#0", lambda: deepen(0))
     SC("red_wait", collect)
     packed = jnp.sum(slots[...], axis=0)
 
@@ -488,6 +660,8 @@
     small, order = ITERS * blk, (ITERS + 1) * blk
     inv = 1.0 / SCALE
 
+    wide = lambda x: jnp.broadcast_to(x, (1, 128))
+
     def solve():
         second = (
             (inv * inv) * left_by(moments, 2 * blk)
@@ -504,10 +678,22 @@
             axis=0,
         )
         rows_small = lax.broadcasted_iota(jnp.int32, (small, 1), 0)
-        for k in range(small):
-            row = normal[k:k + 1] / normal[k:k + 1, k:k + 1]
-            column = jnp.where(rows_small == k, 0.0, normal[:, k:k + 1])
-            normal = jnp.where(rows_small == k, row, normal - column * row)
+        for k in range(0, small, 2):
+            top, low = normal[k:k + 1], normal[k + 1:k + 2]
+            top_k, top_l = wide(top[:, k:k + 1]), wide(top[:, k + 1:k + 2])
+            low_k, low_l = wide(low[:, k:k + 1]), wide(low[:, k + 1:k + 2])
+            inv_top = 1.0 / top_k
+            ratio = low_k * inv_top
+            inv_low = 1.0 / (low_l - ratio * top_l)
+            second_row = (low - ratio * top) * inv_low
+            first_row = (top - top_l * second_row) * inv_top
+            pair = (rows_small == k) | (rows_small == k + 1)
+            first_col = jnp.where(pair, 0.0, normal[:, k:k + 1])
+            second_col = jnp.where(pair, 0.0, normal[:, k + 1:k + 2])
+            rest = normal - first_col * first_row - second_col * second_row
+            normal = jnp.where(
+                rows_small == k, first_row, jnp.where(rows_small == k + 1, second_row, rest)
+            )
         return normal
 
     normal = SC("solve", solve)
@@ -520,10 +706,20 @@
         )
         full = full + jnp.where(lane32 == row32 + order, 1.0, 0.0)
         rows_full = lax.broadcasted_iota(jnp.int32, (order, 1), 0)
-        for k in range(order):
-            row = full[k:k + 1] / full[k:k + 1, k:k + 1]
-            column = jnp.where(rows_full <= k, 0.0, full[:, k:k + 1])
-            full = full - column * row
+        for k in range(0, order, 2):
+            top, low = full[k:k + 1], full[k + 1:k + 2]
+            top_k, top_l = wide(top[:, k:k + 1]), wide(top[:, k + 1:k + 2])
+            low_k, low_l = wide(low[:, k:k + 1]), wide(low[:, k + 1:k + 2])
+            inv_top = 1.0 / top_k
+            ratio = low_k * inv_top
+            left_over = low - ratio * top
+            second_row = left_over * (1.0 / (low_l - ratio * top_l))
+            first_row = (top - top_l * second_row) * inv_top
+            done = rows_full <= k + 1
+            first_col = jnp.where(done, 0.0, full[:, k:k + 1])
+            second_col = jnp.where(done, 0.0, full[:, k + 1:k + 2])
+            rest = full - first_col * first_row - second_col * second_row
+            full = jnp.where(rows_full == k + 1, left_over, rest)
         pivots = jnp.sum(jnp.where(lane32 == row32, full, 0.0), axis=1, keepdims=True)
         full = full / jnp.sqrt(pivots)
         upper = jnp.where((lane32 < order) & (lane32 >= row32), full, 0.0)
@@ -544,11 +740,11 @@
 
     SC("splat", spread)
 
-    def combine(dst, layers, row_start, height, sources):
+    def combine(dst, first_layer, count, row_start, height, sources):
         tiles = height // 8
 
         def run(i, carry):
-            layer, t = layers[0] + i // tiles, i % tiles
+            layer, t = first_layer + i // tiles, i % tiles
             at = pl.multiple_of(row_start + t * 8, 8)
             for lane_at in range(lanes):
                 cols = pl.ds(lane_at * 128, 128)
@@ -567,20 +763,26 @@
                     dst[u, layer, pl.ds(at, 8), cols] = total
             return carry
 
-        lax.fori_loop(0, (layers[1] - layers[0]) * tiles, run, 0)
+        lax.fori_loop(0, count * tiles, run, 0)
 
     def send_late():
         for layer in range(lay):
-            combine(
-                held, (layer, layer + 1), 0, late[layer],
-                [(k, 1 + theirs_at, early[layer]) for k in basis[:ITERS]],
-            )
-            late_copy(layer, hs).start()
+            for first in range(0, late[layer], 8):
+                combine(
+                    held, layer, 1, first, 8,
+                    [
+                        (k, 1 + theirs_at, theirs_out + early[layer] + first)
+                        for k in basis[:ITERS]
+                    ],
+                )
+                late_copy(layer, hs + theirs_out, first, 8).start()
 
     SC("comb_late", send_late)
+    SC("deepen#1", lambda: deepen(1))
     SC("comb_own", lambda: combine(
-        out_ref, (0, lay), hs, half, ((r_ref, 0, hs), (k1, 1 + mine_at, 0), (k2, 1 + mine_at, 0))
+        out_ref, 0, lay, hs, half, ((r_ref, 0, hs), (k1, 1 + mine_at, 0), (k2, 1 + mine_at, 0))
     ))
+    SC("deepen#2", lambda: deepen(2))
 
     def back_wait():
         for layer in range(lay):
@@ -591,41 +793,69 @@
     def rest():
         for layer in range(lay):
             combine(
-                out_ref, (layer, layer + 1), os, early[layer],
-                ((r_ref, 0, os), (ret.at[0, layer], None, 0), (ret.at[1, layer], None, 0)),
+                out_ref, layer, 1, os + mine_out, early[layer],
+                (
+                    (r_ref, 0, os + mine_out),
+                    (ret.at[0, layer], None, 0), (ret.at[1, layer], None, 0),
+                ),
             )
 
     SC("comb_other", rest)
+    SC("deepen#3", lambda: deepen(3))
     SC("factor", factor)
+    SC("deepen#4", lambda: deepen(4))
+
+    def finish_inner():
+        for slot, layer in ((0, far), (1, near_l)):
+            combine(
+                out_ref, layer, 1, inner_at, inner,
+                ((r_ref, 0, inner_at), (kd1.at[slot], None, 0), (kd2.at[slot], None, 0)),
+            )
+
+    SC("comb_inner", finish_inner)
 
     def drain():
         whole = r_ref.at[:, :, pl.ds(os, half)]
         remote(whole, whole, x_s, x_r.at[0, 0], (partner, gy)).wait_send()
-        for j in range(ITERS):
-            for direction, there in ((0, below), (1, above)):
-                @pl.when(there)
-                def _():
-                    every = basis[j].at[:, pl.ds(0, 1)]
-                    remote(
-                        every, every, z_s.at[j, direction], z_r.at[j, direction, 0], (partner, gy)
-                    ).wait_send()
-
-            for side in range(2):
-                @pl.when(has(j, side))
-                def _():
-                    every = ys.at[j, side]
-                    remote(
-                        every, every, y_s.at[j, side], y_r.at[j, side, 0], (partner, gy)
-                    ).wait_send()
+        for direction, there in ((0, below), (1, above)):
+            @pl.when(there)
+            def _():
+                every = k0.at[:, pl.ds(0, ITERS)]
+                remote(
+                    every, every, z_s.at[direction], z_r.at[0, direction, 0], (partner, gy)
+                ).wait_send()
+
+        for side, there in ((0, before), (1, after)):
+            first = has(0, side)
+
+            @pl.when(first)
+            def _():
+                every = ys.at[:, side]
+                remote(every, every, y_s.at[side], y_r.at[0, side, 0], (partner, gy)).wait_send()
+
+            @pl.when(there & jnp.logical_not(first))
+            def _():
+                every = ys.at[pl.ds(1, ITERS - 1), side]
+                remote(every, every, y_s.at[side], y_r.at[0, side, 0], (partner, gy)).wait_send()
 
         diag_copy.wait_send()
+        every = deep.at[pl.ds(2, 2)]
+        remote(every, every, q_s, q_r.at[0], (partner, gy)).wait_send()
+        ghost_copies[0].wait_send()
+        ghost_diag.wait_send()
+
+        @pl.when(onward)
+        def _():
+            remote(every, every, qz_s, qz_r.at[0], (partner, gy)).wait_send()
+            for copy in ghost_relays:
+                copy.wait_send()
 
     SC("drain", drain)
 
     def late_wait():
         for layer in range(lay):
-            late_copy(layer, hs).wait_send()
-            late_copy(layer, os).wait_recv()
+            late_copy(layer, hs + theirs_out, 0, late[layer]).wait_send()
+            late_copy(layer, os + mine_out, 0, late[layer]).wait_recv()
 
     SC("late_wait", late_wait)
 
@@ -644,7 +874,9 @@
 def body(right_side, diagonal):
     blk, lay, rows, nx = right_side.shape
     half, group_lay = rows // 2, 2 * lay
-    early = [half * EARLY[layer % len(EARLY)] // 32 * 8 for layer in range(lay)]
+    inner = half // 2
+    outer = half - inner
+    early = [outer * EARLY[layer % len(EARLY)] // 16 * 8 for layer in range(lay)]
     n_z, n_y = lax.axis_size("gz"), lax.axis_size("gy")
     vmem = lambda *shape: pltpu.VMEM(shape, jnp.float32)
     dma = lambda *shape: pltpu.SemaphoreType.DMA(shape) if shape else pltpu.SemaphoreType.DMA
@@ -664,11 +896,17 @@
             vmem(blk, group_lay, half, nx),
             vmem(group_lay, half, nx),
             vmem(ITERS - 1, lay, blk, max(early), nx),
-            vmem(blk, lay, half - min(early), nx),
+            vmem(blk, lay, outer - min(early), nx),
             vmem(ITERS, 2, blk, group_lay, nx),
             vmem(ITERS, 2, blk, group_lay, nx),
             vmem(blk, lay, 1, nx),
             vmem(blk, lay, 1, nx),
+            vmem(4, blk, inner, nx),
+            vmem(3, inner, nx),
+            vmem(blk, 2, 1, nx),
+            vmem(blk, 3, 1, nx),
+            vmem(2, blk, inner, nx),
+            vmem(2, blk, inner, nx),
             vmem(8 * blk * blk, 128),
             vmem(4, 128),
             vmem(n_z * n_y, 4, 128),
@@ -676,11 +914,12 @@
             dma(CHUNKS + 1), pltpu.SemaphoreType.REGULAR((4,)),
             dma(), dma(2, CHUNKS),
             dma(), dma(),
-            dma(ITERS, 2), dma(ITERS, 2, CHUNKS),
-            dma(ITERS, 2), dma(ITERS, 2, CHUNKS),
+            dma(2), dma(2, 2, CHUNKS),
+            dma(2), dma(2, 2, CHUNKS),
             dma(), dma(),
             dma(lay), dma(lay), dma(lay), dma(lay),
             dma(), dma(),
+            dma(), dma(CHUNKS), dma(), dma(CHUNKS), dma(4), dma(4),
         ],
         compiler_params=pltpu.CompilerParams(
             collective_id=0, has_side_effects=True, vmem_limit_bytes=40 * 1024 * 1024

time: 74.5 us -> 70.6 us (0.948)
  Pallas kernels: 73.7 us -> 69.9 us
    pallas_call x1, Pallas kernels: 72.3 us -> 68.5 us  [body(): pl.pallas_call(kernel, out_shape=(vmem(*right_side.shape), vmem(small, or...]
where the time goes in v3:
time: 70.6 us; the launch traced here: 70.5 us
  Pallas kernels  69.9 us (99%)
    pallas_call x1, Pallas kernels, body(): pl.pallas_call(kernel, out_shape=(vmem(*right_side.shape), vmem(small, or...  68.5 us

profile of v3, /device:TPU:0, one launch (start us, length us, event | category | flops | bytes accessed | tf_op | source)
XLA Modules:
  0.0 70.5 jit_solution(1658706307044240600)
XLA Ops:
  0.6 68.5 %gmres.1 = (f32[8,2,64,512]{3,2,1,0:T(8,128)S(1)}, f32[24,32]{1,0:T(8,128)S(1)}) custom-call(f32[8,2,64,512]{3,2,1,0:T(8,128)} %r_hbm.1, f32[2,64,512]{2,1,0:T(8,128)} %d_hbm.1), custom_call_target="tpu_custom_call" | custom-call | tf_op jit(solution)/shard_map/gmres/pallas_call | solution.py:885
  69.1 1.3 %store.1 = (f32[8,2,64,512]{3,2,1,0:T(8,128)}, f32[24,32]{1,0:T(8,128)}) custom-call(f32[8,2,64,512]{3,2,1,0:T(8,128)S(1)} %get-tuple-element.4.x_ref, f32[24,32]{1,0:T(8,128)S(1)} %get-tuple-element.5.h_ref), custom_call_target="tpu_custom_call" | custom-call | tf_op jit(solution)/shard_map/store/pallas_call | solution.py:930

commit v4 on v3

--- a/solution.py
+++ b/solution.py
@@ -170,7 +170,7 @@
             dst, dev = k0.at[vs, pl.ds(0, 1)], (gz + 2, gy)
         return remote(
             r_ref.at[vs, pl.ds(edge, 1), pl.ds(hs, half)], dst,
-            z_s.at[direction], z_r.at[0, direction, ch], dev,
+            z_s.at[direction], z_r.at[0, ch], dev,
         )
 
     def z_copy(j, ch, direction):
@@ -180,22 +180,15 @@
             src, dst, dev = k.at[vs, pl.ds(1, 1)], k.at[vs, pl.ds(group_lay + 1, 1)], (gz - 2, gy)
         else:
             src, dst, dev = k.at[vs, pl.ds(group_lay, 1)], k.at[vs, pl.ds(0, 1)], (gz + 2, gy)
-        return remote(src, dst, z_s.at[direction], z_r.at[j % 2, direction, ch], dev)
+        return remote(src, dst, z_s.at[direction], z_r.at[j % 2, ch], dev)
 
     def y_copy(j, ch, side):
         vs = part(ch)
         dev = prev_dev if side == 0 else next_dev
         return remote(
             ys.at[j, side, vs], yh.at[j, 1 - side, vs],
-            y_s.at[side], y_r.at[j % 2, 1 - side, ch], dev,
-        )
-
-    def y_wait_recv(j, ch, side):
-        vs = part(ch)
-        remote(
-            ys.at[j, side, vs], yh.at[j, side, vs], y_s.at[side], y_r.at[j % 2, side, ch],
-            (partner, gy),
-        ).wait_recv()
+            y_s.at[side], y_r.at[j % 2, ch], dev,
+        )
 
     def has(j, side):
         if side == 0:
@@ -304,8 +297,11 @@
             z_from_rhs(ch, 1).start()
 
     for v in range(blk):
-        rows_out[v] = jnp.where(
+        rows_out[v, :lay] = jnp.where(
             h == 0, r_ref[v, :, half - 1:half], r_ref[v, :, half:half + 1]
+        )
+        rows_out[v, lay] = jnp.where(
+            h == 0, r_ref[v, near_l, rows - 1:rows], r_ref[v, near_l, 0:1]
         )
         for slot, layer in ((0, near_l), (1, far)):
             g_out[v, slot] = jnp.where(
@@ -417,14 +413,6 @@
             x_s, x_r.at[1, ch], (partner, gy),
         ).wait_recv()
 
-        def run(v, carry):
-            for layer in range(group_lay):
-                stage_rows(0, v, layer, k0[v, 1 + layer])
-            return carry
-
-        lax.fori_loop(starts[ch], starts[ch + 1], run, 0)
-        start_rows(0, ch)
-
     for ch in range(CHUNKS):
         if ch < len(sides):
             SC(f"wave#{ch}", lambda: wave(ch))
@@ -436,12 +424,25 @@
             near = jnp.where(
                 h == 0, r_ref[v, :, half:half + 1], r_ref[v, :, half - 1:half]
             ).reshape(lay, nx)
-            far = rows_in[v].reshape(lay, nx)
-            yh[0, 1 - h, v] = jnp.where(
+            own_row = jnp.where(
+                h == 0, r_ref[v, :, 0:1], r_ref[v, :, rows - 1:rows]
+            ).reshape(lay, nx)
+            both = lambda own, other: jnp.where(
                 p == 0,
-                jnp.concatenate([near, far], axis=0),
-                jnp.concatenate([far, near], axis=0),
-            )
+                jnp.concatenate([own, other], axis=0),
+                jnp.concatenate([other, own], axis=0),
+            )
+            yh[0, 1 - h, v] = both(near, rows_in[v, :lay].reshape(lay, nx))
+            last = 1 + (group_lay - 1) * (1 - p)
+            edge_row = jnp.where(h == 0, k0[v, last, 0:1], k0[v, last, half - 1:half])
+            next_row = rows_in[v, lay]
+            ys[0, h, v] = both(own_row, jnp.where(
+                p == 0,
+                jnp.concatenate([next_row, edge_row], axis=0),
+                jnp.concatenate([edge_row, next_row], axis=0),
+            ))
+        for ch in range(CHUNKS):
+            start_rows(0, ch)
         remote(
             d_ref.at[:, pl.ds(os, half)], diag.at[pl.ds(theirs_at, lay)], d_s, d_r, (partner, gy)
         ).wait_recv()
@@ -456,26 +457,18 @@
         shift = 0 if j == ITERS - 1 else 1
         vs = part(ch)
 
+        def take(there, every, semaphore):
+            for count in (1, 2):
+                @pl.when(there[0].astype(jnp.int32) + there[1].astype(jnp.int32) == count)
+                def _():
+                    ref = every(count)
+                    remote(ref, ref, z_s.at[0], semaphore, (partner, gy)).wait_recv()
+
         def waits():
-            @pl.when(below)
-            def _():
-                remote(
-                    src.at[vs, pl.ds(1, 1)], src.at[vs, pl.ds(0, 1)],
-                    z_s.at[1], z_r.at[j % 2, 1, ch], (partner, gy),
-                ).wait_recv()
-
-            @pl.when(above)
-            def _():
-                remote(
-                    src.at[vs, pl.ds(1, 1)], src.at[vs, pl.ds(group_lay + 1, 1)],
-                    z_s.at[0], z_r.at[j % 2, 0, ch], (partner, gy),
-                ).wait_recv()
+            take((below, above), lambda n: src.at[vs, pl.ds(0, n)], z_r.at[j % 2, ch])
 
         def row_waits():
-            for side in range(2):
-                @pl.when(has(j, side))
-                def _():
-                    y_wait_recv(j, ch, side)
+            take((has(j, 0), has(j, 1)), lambda n: yh.at[j, pl.ds(0, n), vs], y_r.at[j % 2, ch])
 
         for which in RELAY.get((j, ch), ()):
             SC(f"drelay#{which}", lambda: relay_deep(which))
@@ -822,7 +815,7 @@
             def _():
                 every = k0.at[:, pl.ds(0, ITERS)]
                 remote(
-                    every, every, z_s.at[direction], z_r.at[0, direction, 0], (partner, gy)
+                    every, every, z_s.at[direction], z_r.at[0, 0], (partner, gy)
                 ).wait_send()
 
         for side, there in ((0, before), (1, after)):
@@ -831,12 +824,12 @@
             @pl.when(first)
             def _():
                 every = ys.at[:, side]
-                remote(every, every, y_s.at[side], y_r.at[0, side, 0], (partner, gy)).wait_send()
+                remote(every, every, y_s.at[side], y_r.at[0, 0], (partner, gy)).wait_send()
 
             @pl.when(there & jnp.logical_not(first))
             def _():
                 every = ys.at[pl.ds(1, ITERS - 1), side]
-                remote(every, every, y_s.at[side], y_r.at[0, side, 0], (partner, gy)).wait_send()
+                remote(every, every, y_s.at[side], y_r.at[0, 0], (partner, gy)).wait_send()
 
         diag_copy.wait_send()
         every = deep.at[pl.ds(2, 2)]
@@ -899,8 +892,8 @@
             vmem(blk, lay, outer - min(early), nx),
             vmem(ITERS, 2, blk, group_lay, nx),
             vmem(ITERS, 2, blk, group_lay, nx),
-            vmem(blk, lay, 1, nx),
-            vmem(blk, lay, 1, nx),
+            vmem(blk, lay + 1, 1, nx),
+            vmem(blk, lay + 1, 1, nx),
             vmem(4, blk, inner, nx),
             vmem(3, inner, nx),
             vmem(blk, 2, 1, nx),
@@ -914,8 +907,8 @@
             dma(CHUNKS + 1), pltpu.SemaphoreType.REGULAR((4,)),
             dma(), dma(2, CHUNKS),
             dma(), dma(),
-            dma(2), dma(2, 2, CHUNKS),
-            dma(2), dma(2, 2, CHUNKS),
+            dma(2), dma(2, CHUNKS),
+            dma(2), dma(2, CHUNKS),
             dma(), dma(),
             dma(lay), dma(lay), dma(lay), dma(lay),
             dma(), dma(),

time: 70.6 us -> 68.8 us (0.975)
  Pallas kernels: 69.9 us -> 68 us
    pallas_call x1, Pallas kernels: 68.5 us -> 66.7 us  [body(): pl.pallas_call(kernel, out_shape=(vmem(*right_side.shape), vmem(small, or...]
where the time goes in v4:
time: 68.8 us; the launch traced here: 68.6 us
  Pallas kernels  68 us (99%)
    pallas_call x1, Pallas kernels, body(): pl.pallas_call(kernel, out_shape=(vmem(*right_side.shape), vmem(small, or...  66.7 us

profile of v4, /device:TPU:0, one launch (start us, length us, event | category | flops | bytes accessed | tf_op | source)
XLA Modules:
  0.0 68.6 jit_solution(14082613080219683076)
XLA Ops:
  0.6 66.7 %gmres.1 = (f32[8,2,64,512]{3,2,1,0:T(8,128)S(1)}, f32[24,32]{1,0:T(8,128)S(1)}) custom-call(f32[8,2,64,512]{3,2,1,0:T(8,128)} %r_hbm.1, f32[2,64,512]{2,1,0:T(8,128)} %d_hbm.1), custom_call_target="tpu_custom_call" | custom-call | tf_op jit(solution)/shard_map/gmres/pallas_call | solution.py:878
  67.3 1.3 %store.1 = (f32[8,2,64,512]{3,2,1,0:T(8,128)}, f32[24,32]{1,0:T(8,128)}) custom-call(f32[8,2,64,512]{3,2,1,0:T(8,128)S(1)} %get-tuple-element.4.x_ref, f32[24,32]{1,0:T(8,128)S(1)} %get-tuple-element.5.h_ref), custom_call_target="tpu_custom_call" | custom-call | tf_op jit(solution)/shard_map/store/pallas_call | solution.py:923

commit v5 on v4

--- a/solution.py
+++ b/solution.py
@@ -13,12 +13,9 @@
 CUTS = (0, 1, 3, 5, 7, 8)
 CHUNKS = len(CUTS) - 1
 EARLY = (1, 1)
-BACK = {
-    (0, 1): ("ghost",), (0, 2): ((0, 0),), (0, 3): ((0, 1),), (0, 4): ((0, 2),), (1, 1): ((0, 3),),
-    (1, 4): ((0, 4), (1, 0)), (2, 0): ((1, 1),), (2, 1): ((1, 2),),
-    "reduce": ((1, 3), (1, 4), (2, 0), (2, 1), (2, 2), (2, 3), (2, 4)),
-}
-RELAY = {(2, 1): (0,), "reduce": (1, 2, 3, 4)}
+WIDE = (4, 4)
+BACK = {(0, 1): ("ghost",), (0, 2): ((0, 0),), (0, 3): ((0, 1),), (0, 4): ((0, 2),), (1, 1): ((0, 3),), (1, 4): ((0, 4), (1, 0)), (2, 0): ((1, 1),), (2, 1): ((1, 2),), "reduce": ((1, 3), (1, 4), (2, 0), (2, 1), (2, 2), (2, 3), (2, 4))}
+RELAY = {"reduce": (0, 1, 2, 3, 4)}
 MESH = pl.DeviceIdType.MESH
 HIGH = lax.Precision.HIGHEST
 
@@ -42,7 +39,7 @@
     r_hbm, d_hbm, out_ref, hess_ref,
     r_ref, d_ref, k0, k1, k2, k3, diag, ret, held, ys, yh, rows_out, rows_in,
     deep, d_deep, g_out, g_in, kd1, kd2,
-    acc, mine, slots, splat, i_s, met,
+    acc, mine, slots, splat, columns, i_s, met,
     x_s, x_r, d_s, d_r, z_s, z_r, y_s, y_r, e_s, e_r, b_s, b_r, l_s, l_r, g_s, g_r,
     q_s, q_r, qz_s, qz_r, w_s, w_r,
 ):
@@ -72,6 +69,7 @@
     outer = half - inner
     early = [outer * EARLY[layer % len(EARLY)] // 16 * 8 for layer in range(lay)]
     late = [outer - e for e in early]
+    width = [nx * WIDE[layer % len(WIDE)] // 4 for layer in range(lay)]
     theirs_out = pl.multiple_of(h * inner, 8)
     mine_out = pl.multiple_of((1 - h) * inner, 8)
     inner_at = pl.multiple_of(os + h * outer, 8)
@@ -199,25 +197,29 @@
         vs = part(ch)
         return [
             remote(
-                basis[j].at[vs, 1 + theirs_at + layer, pl.ds(theirs_out, early[layer])],
-                ret.at[j - 1, layer, vs, pl.ds(0, early[layer])],
+                basis[j].at[vs, 1 + theirs_at + layer, pl.ds(theirs_out, early[layer]), pl.ds(0, width[layer])],
+                ret.at[j - 1, layer, vs, pl.ds(0, early[layer]), pl.ds(0, width[layer])],
                 b_s.at[layer], b_r.at[layer], (partner, gy),
             )
             for layer in range(lay)
         ]
 
     def all_back(layer):
-        every = ret.at[:, layer, :, pl.ds(0, early[layer])]
+        every = ret.at[:, layer, :, pl.ds(0, early[layer]), pl.ds(0, width[layer])]
         return remote(every, every, b_s.at[layer], b_r.at[layer], (partner, gy))
 
-    def late_copy(layer, at, first, count):
+    def late_copy(layer, at, first, count, lane_at, sem):
+        cols = pl.ds(lane_at, nx - lane_at)
         return remote(
-            held.at[:, pl.ds(layer, 1), pl.ds(first, count)],
-            out_ref.at[
-                :, pl.ds(layer, 1), pl.ds(pl.multiple_of(at + early[layer] + first, 8), count)
-            ],
-            l_s.at[layer], l_r.at[layer], (partner, gy),
-        )
+            held.at[:, pl.ds(layer, 1), pl.ds(first, count), cols],
+            out_ref.at[:, pl.ds(layer, 1), pl.ds(pl.multiple_of(at + first, 8), count), cols],
+            l_s.at[sem], l_r.at[sem], (partner, gy),
+        )
+
+    late_parts = [
+        (layer, 0, early[layer], width[layer], lay + layer)
+        for layer in range(lay) if width[layer] < nx
+    ] + [(layer, early[layer], late[layer], 0, layer) for layer in range(lay) if late[layer]]
 
     give_at = pl.multiple_of(hs + (1 - h) * outer, 8)
 
@@ -624,12 +626,16 @@
         mine[...] = packed
         slots[me] = packed
 
-        def send(off, carry):
-            to = (me + off) % n_dev
-            remote(mine, slots.at[me], g_s, g_r, device(to)).start()
+        def send(i, carry):
+            to = jnp.where(2 * gz < n_z, n_dev - 1 - i, i)
+
+            @pl.when(to != me)
+            def _():
+                remote(mine, slots.at[me], g_s, g_r, device(to)).start()
+
             return carry
 
-        lax.fori_loop(1, n_dev, send, 0)
+        lax.fori_loop(0, n_dev, send, 0)
         issue(BACK.get("reduce", ()))
         for which in RELAY.get("reduce", ()):
             relay_deep(which)
@@ -640,7 +646,6 @@
         others = slots.at[pl.ds(0, n_dev - 1)]
         remote(others, others, g_s, g_r, (partner, gy)).wait()
 
-    SC("deepen#0", lambda: deepen(0))
     SC("red_wait", collect)
     packed = jnp.sum(slots[...], axis=0)
 
@@ -725,22 +730,22 @@
         hess_ref[...] = jnp.where(col_h // blk <= row_h // blk + 1, hess, 0.0)
 
     def spread():
+        for u in range(blk):
+            columns[u] = jnp.broadcast_to(normal[:, small + u:small + u + 1], (small, 128))
         for k in range(small):
             for u in range(blk):
-                splat[k * blk + u] = jnp.broadcast_to(
-                    normal[k:k + 1, small + u:small + u + 1], (8, 128)
-                )
+                splat[k * blk + u] = jnp.broadcast_to(columns[u, k:k + 1], (8, 128))
 
     SC("splat", spread)
 
-    def combine(dst, first_layer, count, row_start, height, sources):
+    def combine(dst, first_layer, count, row_start, height, sources, low=0, high=None):
         tiles = height // 8
 
         def run(i, carry):
             layer, t = first_layer + i // tiles, i % tiles
             at = pl.multiple_of(row_start + t * 8, 8)
-            for lane_at in range(lanes):
-                cols = pl.ds(lane_at * 128, 128)
+            for lane_at in range(low, nx if high is None else high, 128):
+                cols = pl.ds(lane_at, 128)
                 vals = []
                 for ref, l_at, base in sources:
                     first_row = pl.multiple_of(base + t * 8, 8)
@@ -759,23 +764,22 @@
         lax.fori_loop(0, count * tiles, run, 0)
 
     def send_late():
-        for layer in range(lay):
-            for first in range(0, late[layer], 8):
+        for layer, start, count, lane_at, sem in late_parts:
+            for first in range(start, start + count, 8):
                 combine(
                     held, layer, 1, first, 8,
-                    [
-                        (k, 1 + theirs_at, theirs_out + early[layer] + first)
-                        for k in basis[:ITERS]
-                    ],
+                    [(k, 1 + theirs_at, theirs_out + first) for k in basis[:ITERS]], lane_at,
                 )
-                late_copy(layer, hs + theirs_out, first, 8).start()
+                late_copy(layer, hs + theirs_out, first, 8, lane_at, sem).start()
 
     SC("comb_late", send_late)
-    SC("deepen#1", lambda: deepen(1))
+    for ch in range(2):
+        SC(f"deepen#{ch}", lambda: deepen(ch))
     SC("comb_own", lambda: combine(
         out_ref, 0, lay, hs, half, ((r_ref, 0, hs), (k1, 1 + mine_at, 0), (k2, 1 + mine_at, 0))
     ))
     SC("deepen#2", lambda: deepen(2))
+    SC("factor", factor)
 
     def back_wait():
         for layer in range(lay):
@@ -791,12 +795,13 @@
                     (r_ref, 0, os + mine_out),
                     (ret.at[0, layer], None, 0), (ret.at[1, layer], None, 0),
                 ),
+                0, width[layer],
             )
 
     SC("comb_other", rest)
     SC("deepen#3", lambda: deepen(3))
-    SC("factor", factor)
-    SC("deepen#4", lambda: deepen(4))
+    for ch in range(4, CHUNKS):
+        SC(f"deepen#{ch}", lambda: deepen(ch))
 
     def finish_inner():
         for slot, layer in ((0, far), (1, near_l)):
@@ -846,9 +851,9 @@
     SC("drain", drain)
 
     def late_wait():
-        for layer in range(lay):
-            late_copy(layer, hs + theirs_out, 0, late[layer]).wait_send()
-            late_copy(layer, os + mine_out, 0, late[layer]).wait_recv()
+        for layer, start, count, lane_at, sem in late_parts:
+            late_copy(layer, hs + theirs_out, start, count, lane_at, sem).wait_send()
+            late_copy(layer, os + mine_out, start, count, lane_at, sem).wait_recv()
 
     SC("late_wait", late_wait)
 
@@ -889,7 +894,7 @@
             vmem(blk, group_lay, half, nx),
             vmem(group_lay, half, nx),
             vmem(ITERS - 1, lay, blk, max(early), nx),
-            vmem(blk, lay, outer - min(early), nx),
+            vmem(blk, lay, outer, nx),
             vmem(ITERS, 2, blk, group_lay, nx),
             vmem(ITERS, 2, blk, group_lay, nx),
             vmem(blk, lay + 1, 1, nx),
@@ -904,13 +909,14 @@
             vmem(4, 128),
             vmem(n_z * n_y, 4, 128),
             vmem(small * blk, 8, 128),
+            vmem(blk, small, 128),
             dma(CHUNKS + 1), pltpu.SemaphoreType.REGULAR((4,)),
             dma(), dma(2, CHUNKS),
             dma(), dma(),
             dma(2), dma(2, CHUNKS),
             dma(2), dma(2, CHUNKS),
             dma(), dma(),
-            dma(lay), dma(lay), dma(lay), dma(lay),
+            dma(lay), dma(lay), dma(2 * lay), dma(2 * lay),
             dma(), dma(),
             dma(), dma(CHUNKS), dma(), dma(CHUNKS), dma(4), dma(4),
         ],

time: 68.8 us -> 68.4 us (level)
  no operation moved by 1% of the time
where the time goes in v5:
time: 68.4 us; the launch traced here: 68.3 us
  Pallas kernels  67.6 us (99%)
    pallas_call x1, Pallas kernels, body(): pl.pallas_call(kernel, out_shape=(vmem(*right_side.shape), vmem(small, or...  66.3 us

profile of v5, /device:TPU:0, one launch (start us, length us, event | category | flops | bytes accessed | tf_op | source)
XLA Modules:
  0.0 68.3 jit_solution(9613504194968135258)
XLA Ops:
  0.6 66.3 %gmres.1 = (f32[8,2,64,512]{3,2,1,0:T(8,128)S(1)}, f32[24,32]{1,0:T(8,128)S(1)}) custom-call(f32[8,2,64,512]{3,2,1,0:T(8,128)} %r_hbm.1, f32[2,64,512]{2,1,0:T(8,128)} %d_hbm.1), custom_call_target="tpu_custom_call" | custom-call | tf_op jit(solution)/shard_map/gmres/pallas_call | solution.py:883
  66.9 1.3 %store.1 = (f32[8,2,64,512]{3,2,1,0:T(8,128)}, f32[24,32]{1,0:T(8,128)}) custom-call(f32[8,2,64,512]{3,2,1,0:T(8,128)S(1)} %get-tuple-element.4.x_ref, f32[24,32]{1,0:T(8,128)S(1)} %get-tuple-element.5.h_ref), custom_call_target="tpu_custom_call" | custom-call | tf_op jit(solution)/shard_map/store/pallas_call | solution.py:929

commit v6 on v5

--- a/solution.py
+++ b/solution.py
@@ -14,7 +14,7 @@
 CHUNKS = len(CUTS) - 1
 EARLY = (1, 1)
 WIDE = (4, 4)
-BACK = {(0, 1): ("ghost",), (0, 2): ((0, 0),), (0, 3): ((0, 1),), (0, 4): ((0, 2),), (1, 1): ((0, 3),), (1, 4): ((0, 4), (1, 0)), (2, 0): ((1, 1),), (2, 1): ((1, 2),), "reduce": ((1, 3), (1, 4), (2, 0), (2, 1), (2, 2), (2, 3), (2, 4))}
+BACK = {(0, 2): ((0, 0),), (0, 3): ((0, 1),), (0, 4): ((0, 2),), (1, 2): ((0, 3),), (1, 4): ("ghost", (0, 4), (1, 0)), (2, 0): ((1, 1),), (2, 1): ((1, 2),), "reduce": ((1, 3), (1, 4), (2, 0), (2, 1), (2, 2), (2, 3), (2, 4))}
 RELAY = {"reduce": (0, 1, 2, 3, 4)}
 MESH = pl.DeviceIdType.MESH
 HIGH = lax.Precision.HIGHEST
@@ -228,14 +228,13 @@
         return [
             remote(
                 r_ref.at[vs, layer, pl.ds(give_at, inner)], deep.at[slot, vs],
-                q_s, q_r.at[ch], (partner, gy),
+                q_s, q_r, (partner, gy),
             )
             for slot, layer in ((2, near_l), (3, far))
         ]
 
-    def deep_recv(ch):
-        every = deep.at[pl.ds(2, 2), part(ch)]
-        return remote(every, every, q_s, q_r.at[ch], (partner, gy))
+    every_deep = deep.at[pl.ds(2, 2)]
+    all_deep = remote(every_deep, every_deep, q_s, q_r, (partner, gy))
 
     def deep_relay(ch):
         vs = part(ch)
@@ -269,8 +268,8 @@
                 copy.start()
 
     def relay_deep(ch):
-        deep_recv(ch).wait_recv()
         if ch == 0:
+            all_deep.wait_recv()
             ghost_copies[0].wait_recv()
             ghost_diag.wait_recv()
 
@@ -838,7 +837,7 @@
 
         diag_copy.wait_send()
         every = deep.at[pl.ds(2, 2)]
-        remote(every, every, q_s, q_r.at[0], (partner, gy)).wait_send()
+        all_deep.wait_send()
         ghost_copies[0].wait_send()
         ghost_diag.wait_send()
 
@@ -876,6 +875,7 @@
     outer = half - inner
     early = [outer * EARLY[layer % len(EARLY)] // 16 * 8 for layer in range(lay)]
     n_z, n_y = lax.axis_size("gz"), lax.axis_size("gy")
+    parts = 2 * lay if min(WIDE) < 4 else lay
     vmem = lambda *shape: pltpu.VMEM(shape, jnp.float32)
     dma = lambda *shape: pltpu.SemaphoreType.DMA(shape) if shape else pltpu.SemaphoreType.DMA
     small, order = ITERS * blk, (ITERS + 1) * blk
@@ -916,9 +916,9 @@
             dma(2), dma(2, CHUNKS),
             dma(2), dma(2, CHUNKS),
             dma(), dma(),
-            dma(lay), dma(lay), dma(2 * lay), dma(2 * lay),
+            dma(lay), dma(lay), dma(parts), dma(parts),
             dma(), dma(),
-            dma(), dma(CHUNKS), dma(), dma(CHUNKS), dma(4), dma(4),
+            dma(), dma(), dma(), dma(CHUNKS), dma(4), dma(4),
         ],
         compiler_params=pltpu.CompilerParams(
             collective_id=0, has_side_effects=True, vmem_limit_bytes=40 * 1024 * 1024

time: 68.4 us -> 68.3 us (level)
  no operation moved by 1% of the time
where the time goes in v6:
time: 68.3 us; the launch traced here: 68.2 us
  Pallas kernels  67.6 us (99%)
    pallas_call x1, Pallas kernels, body(): pl.pallas_call(kernel, out_shape=(vmem(*right_side.shape), vmem(small, or...  66.2 us

profile of v6, /device:TPU:0, one launch (start us, length us, event | category | flops | bytes accessed | tf_op | source)
XLA Modules:
  0.0 68.2 jit_solution(10319679213003235669)
XLA Ops:
  0.6 66.2 %gmres.1 = (f32[8,2,64,512]{3,2,1,0:T(8,128)S(1)}, f32[24,32]{1,0:T(8,128)S(1)}) custom-call(f32[8,2,64,512]{3,2,1,0:T(8,128)} %r_hbm.1, f32[2,64,512]{2,1,0:T(8,128)} %d_hbm.1), custom_call_target="tpu_custom_call" | custom-call | tf_op jit(solution)/shard_map/gmres/pallas_call | solution.py:883
  66.9 1.3 %store.1 = (f32[8,2,64,512]{3,2,1,0:T(8,128)}, f32[24,32]{1,0:T(8,128)}) custom-call(f32[8,2,64,512]{3,2,1,0:T(8,128)S(1)} %get-tuple-element.4.x_ref, f32[24,32]{1,0:T(8,128)S(1)} %get-tuple-element.5.h_ref), custom_call_target="tpu_custom_call" | custom-call | tf_op jit(solution)/shard_map/store/pallas_call | solution.py:929
